TPU v7x, 128 devices: a whole 4x4x4 slice. The times are simulated.
128 devices in a mesh: facet: 16 (over y, x_lo, core), col: 8 (over x_hi, z).
Axes of the slice: x: 4 (x_hi: 2, x_lo: 2; x = x_hi * 2 + x_lo), y: 4, z: 4, core: 2. Of those that a mesh axis runs over, the one named last changes fastest.
Arguments:
- sky_image: float32 [2, 2048, 8192], P(None, ('facet', 'col')), may hold values from -6 to 6
- observed: float32 [2, 4096, 2048], P(None, 'facet', 'col'), may hold values from -4 to 4
- weights: int32 [4096, 2048], P('facet', 'col'), may hold values from 0 to 3
- facet_offsets: int32 [16, 2], replicated, may hold values from 0 to 7, as said below
- subgrid_rows: int32 [16], replicated, may hold values from 0 to 65535
- subgrid_columns: int32 [8], replicated, may hold values from 0 to 65535
Outputs:
- new_image: float32 [2, 2048, 8192], P(None, ('facet', 'col'))
- predicted: float32 [2, 4096, 2048], P(None, 'facet', 'col')
Inputs may be any that keep to these rules, and one draw needn't show every extreme that they name: `facet_offsets`: each row is the (row, column) slot of one facet on a 8 x 8 layout; no two facets share a slot.
All inputs are finite; a program needn't handle non-finite values.
Results may differ from a plain program's by a relative error of at most 0.0003.
Values sent between devices are 32-bit elements; how exact they have to be, the bound alone decides.
A program may use at most 128 MiB of HBM per device.

v0:
```python
import math

import jax
import jax.numpy as jnp
from jax import lax
from jax.sharding import PartitionSpec as P

FN = 8192
M = 32
SLOTS = 8
NIMG = 65536
G = 256


HIGHEST = lax.Precision.HIGHEST
shrink_level = 0.5


def product(form, first, second):
    real_part = jnp.einsum(form, first[0], second[0], precision=HIGHEST) - jnp.einsum(
        form, first[1], second[1], precision=HIGHEST
    )
    imag_part = jnp.einsum(form, first[0], second[1], precision=HIGHEST) + jnp.einsum(
        form, first[1], second[0], precision=HIGHEST
    )
    return (real_part, imag_part)


def conjugate(pair):
    return (pair[0], -pair[1])


def phases(first_ids, second_ids, period, extent):
    wrapped = jnp.remainder(first_ids[:, None] * second_ids[None, :], period)
    angles = wrapped.astype(jnp.float32) * (2.0 * math.pi / period)
    factor = 1.0 / math.sqrt(extent)
    return (jnp.cos(angles) * factor, -jnp.sin(angles) * factor)


def shrink(values):
    magnitude = jnp.sqrt(values[0] * values[0] + values[1] * values[1])
    ratio = jnp.maximum(magnitude - shrink_level, 0.0) / jnp.maximum(magnitude, shrink_level)
    return values * ratio[None]


def subgrid_tables(facet_offsets, contrib, grid):
    contrib_ids = jnp.arange(contrib, dtype=jnp.int32)
    grid_ids = jnp.arange(grid, dtype=jnp.int32)
    row_place = (facet_offsets[:, 0:1] * contrib + contrib_ids[None, :]).reshape(-1)
    column_place = (facet_offsets[:, 1:2] * contrib + contrib_ids[None, :]).reshape(-1)
    downward = phases(row_place, grid_ids, grid, grid)
    sideways = phases(column_place, grid_ids, grid, grid)
    sideways = (sideways[0].reshape(-1, contrib, grid), sideways[1].reshape(-1, contrib, grid))
    return (downward, sideways)


def subgrid_predict(parts, tables):
    downward, sideways = tables
    halfway = product("fpq,fqv->fpv", (parts[:, 0], parts[:, 1]), sideways)
    flat = (
        halfway[0].reshape(-1, halfway[0].shape[2]),
        halfway[1].reshape(-1, halfway[1].shape[2]),
    )
    return product("ku,kv->uv", downward, flat)


def subgrid_adjoint(resid, tables):
    downward, sideways = tables
    upper = product("ku,uv->kv", conjugate(downward), resid)
    facet_count = sideways[0].shape[0]
    upper = (
        upper[0].reshape(facet_count, -1, upper[0].shape[1]),
        upper[1].reshape(facet_count, -1, upper[1].shape[1]),
    )
    back = product("fpv,fqv->fpq", upper, conjugate(sideways))
    return jnp.stack(back, axis=1)


def local(sky_image, observed, weights, facet_offsets, subgrid_rows, subgrid_columns):
    facet = lax.axis_index("facet")
    column = lax.axis_index("col")
    width = lax.axis_size("col")
    facet_count = facet_offsets.shape[0]
    slab_rows = sky_image.shape[1]
    frows = slab_rows * width
    row_step = NIMG // frows
    slot = facet_offsets[facet]
    contrib_ids = jnp.arange(M, dtype=jnp.int32)
    row_index = slot[0] * FN + column * slab_rows + jnp.arange(slab_rows, dtype=jnp.int32)
    column_index = slot[1] * FN + jnp.arange(FN, dtype=jnp.int32)
    row_freq = (subgrid_rows[:, None] + row_step * contrib_ids[None, :]).reshape(-1)
    across = phases(row_index, row_freq, NIMG, frows)

    def column_table():
        column_freq = (subgrid_columns[:, None] + SLOTS * contrib_ids[None, :]).reshape(-1)
        return phases(column_index, column_freq, NIMG, FN)

    def partials(facet_slab, amount):
        inner = product("rx,xj->rj", (facet_slab[0], facet_slab[1]), column_table())
        terms = product("ri,rj->ij", across, inner)
        return jnp.stack(terms).reshape(2, facet_count, M, amount, M)

    def gather_terms(facet_slab):
        stacked = (
            partials(facet_slab, width)
            .transpose(1, 3, 0, 2, 4)
            .reshape(facet_count * width, 2, M * M)
        )
        arrived = lax.all_to_all(stacked, ("facet", "col"), split_axis=0, concat_axis=0, tiled=True)
        summed = arrived.reshape(facet_count, width, 2, M * M).sum(axis=1)
        return summed.reshape(facet_count, 2, M, M)

    tables = subgrid_tables(facet_offsets, M, G)
    first_parts = gather_terms(sky_image)
    model = subgrid_predict(first_parts, tables)
    masks = weights.astype(jnp.float32)
    resid = (masks * (observed[0] - model[0]), masks * (observed[1] - model[1]))
    back = subgrid_adjoint(resid, tables).reshape(facet_count, 2, M * M)
    returned = lax.all_to_all(back, "facet", split_axis=0, concat_axis=0, tiled=True)
    portion = lax.all_gather(returned[None], "col", axis=0, tiled=True)
    amount = portion.shape[0]
    matrix = (
        portion.reshape(amount, facet_count, 2, M, M)
        .transpose(2, 1, 3, 0, 4)
        .reshape(2, facet_count * M, amount * M)
    )
    partial_sum = product("ri,ij->rj", conjugate(across), (matrix[0], matrix[1]))
    grads = product("rj,xj->rx", partial_sum, conjugate(column_table()))
    grads = jnp.stack(grads)
    new_image = shrink(sky_image + grads)
    second_parts = gather_terms(new_image)
    predicted = jnp.stack(subgrid_predict(second_parts, tables))
    return (new_image, predicted)


def solution(mesh):
    return jax.shard_map(
        local,
        mesh=mesh,
        in_specs=(
            P(None, ("facet", "col"), None),
            P(None, "facet", "col"),
            P("facet", "col"),
            P(),
            P(),
            P(),
        ),
        out_specs=(P(None, ("facet", "col"), None), P(None, "facet", "col")),
        check_vma=False,
    )
```

profile of v0, /device:TPU:1, one launch (start us, length us, event | category | flops | bytes accessed | tf_op | source)
XLA Modules:
  0.0 776.8 jit_solution(16992218388934180218)
XLA Ops:
  9.9 40.0 %fusion.11 = f32[256,16]{0,1:T(8,128)S(1)} fusion(s32[256]{0:T(256)S(1)} %add.215, s32[8192]{0:T(1024)S(1)} %iota_add_fusion, f32[2,16,8192]{2,1,0:T(8,128)} %param.6), kind=kOutput, calls=%fused_computation.22 | convolution fusion | flops 434110464 | bytes 574464 | tf_op jit(solution)/shard_map/rx,xj->rj/dot_general | solution.py:23
  50.0 35.3 %fusion.12 = f32[256,16]{0,1:T(8,128)S(1)} fusion(s32[256]{0:T(256)S(1)} %add.215, s32[8192]{0:T(1024)S(1)} %iota_add_fusion, f32[2,16,8192]{2,1,0:T(8,128)S(1)} %copy-done.2), kind=kOutput, calls=%fused_computation.23 | convolution fusion | flops 434110464 | bytes 574464 | tf_op jit(solution)/shard_map/rx,xj->rj/dot_general | solution.py:20
  86.1 47.9 %fusion.24 = f32[256,16]{0,1:T(8,128)S(1)} fusion(f32[256,16]{0,1:T(8,128)S(1)} %fusion.11, s32[256]{0:T(256)S(1)} %add.215, s32[8192]{0:T(1024)S(1)} %iota_add_fusion, f32[2,16,8192]{2,1,0:T(8,128)S(1)} %copy-done.2), kind=kOutput, calls=%fused_computation.53 | convolution fusion | flops 436211712 | bytes 590848 | tf_op jit(solution)/shard_map/rx,xj->rj/dot_general | solution.py:23
  134.0 48.2 %fusion.23 = f32[256,16]{0,1:T(8,128)S(1)} fusion(f32[256,16]{0,1:T(8,128)S(1)} %fusion.12, s32[256]{0:T(256)S(1)} %add.215, s32[8192]{0:T(1024)S(1)} %iota_add_fusion, f32[2,16,8192]{2,1,0:T(8,128)S(1)} %copy-done.2), kind=kOutput, calls=%fused_computation.52 | convolution fusion | flops 436211712 | bytes 590848 | tf_op jit(solution)/shard_map/rx,xj->rj/dot_general | solution.py:20
  192.2 3.8 reshape.162
  197.7 11.5 %all-to-all-start = ((f32[128,2,1024]{2,1,0:T(2,128)}), f32[128,2,1024]{2,1,0:T(2,128)S(1)}, u32[]{:S(2)}, u32[]{:S(2)}) async-start(f32[128,2,1024]{2,1,0:T(2,128)} %copy.31), calls=%async_computation | async-start | bytes 2097152 | tf_op jit(solution)/shard_map/all_to_all | solution.py:109
  209.5 18.1 %all-to-all-done = f32[128,2,1024]{2,1,0:T(2,128)S(1)} async-done(((f32[128,2,1024]{2,1,0:T(2,128)}), f32[128,2,1024]{2,1,0:T(2,128)S(1)}, u32[]{:S(2)}, u32[]{:S(2)}) %all-to-all-start) | async-done | bytes 1048608 | tf_op jit(solution)/shard_map/all_to_all | solution.py:109
  228.1 3.3 fusion.58
  234.7 3.3 convolution_add_fusion.5
  238.0 3.5 convolution_subtract_fusion.5
  250.4 3.4 fusion.20
  253.8 3.5 fusion.63
  257.2 3.5 convolution_subtract_fusion.4
  260.7 3.3 fusion.45
  267.4 3.5 fusion.61
  270.8 3.5 convolution_add_fusion.4
  277.6 3.3 convolution_subtract_fusion.7
  281.4 10.8 %all_to_all.15 = f32[16,2,1024]{2,1,0:T(2,128)} all-to-all(f32[16,2,1024]{2,1,0:T(2,128)S(1)} %pad_maximum_fusion.1), channel_id=1, replica_groups=mesh['facet'=16,'col'=8] {'facet'}, dimensions={0} | all-to-all | bytes 262144 | tf_op jit(solution)/shard_map/all_to_all | solution.py:119
  292.3 40.7 %all-gather.3.cloned.1.call-done = f32[128,2,1024]{2,1,0:T(2,128)} async-done(((f32[16,2,1024]{2,1,0:T(2,128)}), f32[128,2,1024]{2,1,0:T(2,128)}) %all-gather.3.cloned.1.call-update) | async-done | bytes 1048592 | tf_op jit(solution)/shard_map/all_gather | solution.py:120
  337.3 4.2 fusion.316
  348.9 50.9 %fusion.5 = f32[16,8192]{1,0:T(8,128)S(1)} fusion(f32[16,256]{1,0:T(8,128)S(1)} %convolution_subtract_fusion.9, s32[256]{0:T(256)S(1)} %add.215, s32[8192]{0:T(1024)S(1)} %iota_add_fusion), kind=kOutput, calls=%fused_computation.14 | convolution fusion | flops 438304768 | bytes 574464 | tf_op jit(solution)/shard_map/rj,xj->rx/dot_general | solution.py:23
  399.8 37.1 %fusion.10 = f32[16,8192]{1,0:T(8,128)S(1)} fusion(f32[16,256]{1,0:T(8,128)S(1)} %convolution_subtract_fusion.9, s32[256]{0:T(256)S(1)} %add.215, s32[8192]{0:T(1024)S(1)} %iota_add_fusion), kind=kOutput, calls=%fused_computation.21 | convolution fusion | flops 434110464 | bytes 574464 | tf_op jit(solution)/shard_map/rj,xj->rx/dot_general | solution.py:20
  437.4 50.2 %fusion = f32[1,16,8192]{2,1,0:T(8,128)S(1)} fusion(f32[16,8192]{1,0:T(8,128)S(1)} %fusion.5, f32[16,256]{1,0:T(8,128)S(1)} %convolution_add_fusion.9, s32[256]{0:T(256)S(1)} %add.215, s32[8192]{0:T(1024)S(1)} %iota_add_fusion), kind=kOutput, calls=%fused_computation.6 | convolution fusion | flops 434241536 | bytes 1098752 | tf_op jit(solution)/shard_map/rj,xj->rx/dot_general | solution.py:23
  487.7 63.2 %fusion.1 = f32[1,16,8192]{2,1,0:T(8,128)S(1)} fusion(f32[16,8192]{1,0:T(8,128)S(1)} %fusion.10, f32[16,256]{1,0:T(8,128)S(1)} %convolution_add_fusion.9, s32[256]{0:T(256)S(1)} %add.215, s32[8192]{0:T(1024)S(1)} %iota_add_fusion), kind=kOutput, calls=%fused_computation.8 | convolution fusion | flops 438435840 | bytes 1098752 | tf_op jit(solution)/shard_map/rj,xj->rx/dot_general | solution.py:20
  551.5 34.1 %fusion.8 = f32[16,256]{1,0:T(8,128)S(1)} fusion(s32[256]{0:T(256)S(1)} %add.215, s32[8192]{0:T(1024)S(1)} %iota_add_fusion, f32[2,16,8192]{2,1,0:T(8,128)S(1)} %broadcast_multiply_fusion), kind=kOutput, calls=%fused_computation.19 | convolution fusion | flops 434110464 | bytes 574464 | tf_op jit(solution)/shard_map/rx,xj->rj/dot_general | solution.py:23
  585.6 46.5 %fusion.9 = f32[16,256]{1,0:T(8,128)S(1)} fusion(s32[256]{0:T(256)S(1)} %add.215, s32[8192]{0:T(1024)S(1)} %iota_add_fusion, f32[2,16,8192]{2,1,0:T(8,128)S(1)} %broadcast_multiply_fusion), kind=kOutput, calls=%fused_computation.20 | convolution fusion | flops 434110464 | bytes 574464 | tf_op jit(solution)/shard_map/rx,xj->rj/dot_general | solution.py:20
  632.1 34.8 %fusion.26 = f32[16,256]{1,0:T(8,128)S(1)} fusion(f32[16,256]{1,0:T(8,128)S(1)} %fusion.8, s32[256]{0:T(256)S(1)} %add.215, s32[8192]{0:T(1024)S(1)} %iota_add_fusion, f32[2,16,8192]{2,1,0:T(8,128)S(1)} %broadcast_multiply_fusion), kind=kOutput, calls=%fused_computation.55 | convolution fusion | flops 436211712 | bytes 590848 | tf_op jit(solution)/shard_map/rx,xj->rj/dot_general | solution.py:23
  666.9 35.0 %fusion.25 = f32[16,256]{1,0:T(8,128)S(1)} fusion(f32[16,256]{1,0:T(8,128)S(1)} %fusion.9, s32[256]{0:T(256)S(1)} %add.215, s32[8192]{0:T(1024)S(1)} %iota_add_fusion, f32[2,16,8192]{2,1,0:T(8,128)S(1)} %broadcast_multiply_fusion), kind=kOutput, calls=%fused_computation.54 | convolution fusion | flops 436211712 | bytes 590848 | tf_op jit(solution)/shard_map/rx,xj->rj/dot_general | solution.py:20
  711.7 3.7 reshape.170
  716.3 26.9 %all_to_all.16 = f32[128,2,1024]{2,1,0:T(2,128)S(1)} all-to-all(f32[128,2,1024]{2,1,0:T(2,128)S(1)} %copy.40), channel_id=1, replica_groups=mesh['facet'=16,'col'=8] {'facet','col'}, dimensions={0} | all-to-all | bytes 2097152 | tf_op jit(solution)/shard_map/all_to_all | solution.py:109
  743.7 3.3 fusion.57
  756.6 3.5 convolution_subtract_fusion.3
  (93 shorter events, 76.9 us)
Async XLA Ops:
  9.9 40.0 %copy-start.2 = (f32[2,16,8192]{2,1,0:T(8,128)S(1)}, f32[2,16,8192]{2,1,0:T(8,128)}, u32[]{:S(2)}) copy-start(f32[2,16,8192]{2,1,0:T(8,128)} %param.6) | copy-start | bytes 3145732
  50.0 35.9 %copy-start.8 = (s32[16]{0:T(128)S(1)}, s32[16]{0:T(128)}, u32[]{:S(2)}) copy-start(s32[16]{0:T(128)} %param.10) | copy-start | bytes 196
  187.9 1.6 copy-start
  192.2 17.1 %copy-start.5 = (s32[16,2]{0,1:T(2,128)S(1)}, s32[16,2]{0,1:T(2,128)}, u32[]{:S(2)}) copy-start(s32[16,2]{0,1:T(2,128)} %param.9) | copy-start | bytes 388
  197.7 29.9 %all-to-all-start = ((f32[128,2,1024]{2,1,0:T(2,128)}), f32[128,2,1024]{2,1,0:T(2,128)S(1)}, u32[]{:S(2)}, u32[]{:S(2)}) async-start(f32[128,2,1024]{2,1,0:T(2,128)} %copy.31), calls=%async_computation | async-start | bytes 2097152 | tf_op jit(solution)/shard_map/all_to_all | solution.py:109
  209.2 123.8 %all-gather.3.cloned.1.call-start = ((), (), s32[]{:S(2)}) async-start(), calls=%async_computation.3 | async-start | bytes 1179648 | tf_op jit(solution)/shard_map/all_gather | solution.py:120
  209.4 61.4 %copy-start.6 = (s32[512]{0:T(512)}, s32[512]{0:T(512)S(1)}, u32[]{:S(2)}) copy-start(s32[512]{0:T(512)S(1)} %add.208) | copy-start | bytes 6148
  238.0 9.4 %copy-start.9 = (f32[2,256,256]{2,1,0:T(8,128)S(1)}, f32[2,256,256]{2,1,0:T(8,128)}, u32[]{:S(2)}) copy-start(f32[2,256,256]{2,1,0:T(8,128)} %param.7) | copy-start | bytes 1572868
  238.0 9.4 %copy-start.10 = (s32[256,256]{1,0:T(8,128)S(1)}, s32[256,256]{1,0:T(8,128)}, u32[]{:S(2)}) copy-start(s32[256,256]{1,0:T(8,128)} %param.8) | copy-start | bytes 786436
  487.6 63.3 %copy-start.3 = (f32[2,16,8192]{2,1,0:T(8,128)S(1)}, f32[2,16,8192]{2,1,0:T(8,128)}, u32[]{:S(2)}) copy-start(f32[2,16,8192]{2,1,0:T(8,128)} %param.6) | copy-start | bytes 3145732
  551.4 115.4 %copy-start.4 = (f32[2,16,8192]{2,1,0:T(8,128)}, f32[2,16,8192]{2,1,0:T(8,128)S(1)}, u32[]{:S(2)}) copy-start(f32[2,16,8192]{2,1,0:T(8,128)S(1)} %broadcast_multiply_fusion) | copy-start | bytes 3145732
  707.5 1.6 copy-start.1
  743.5 10.1 %copy-start.7 = (s32[512]{0:T(512)S(1)}, s32[512]{0:T(512)}, u32[]{:S(2)}) copy-start(s32[512]{0:T(512)} %copy-done.6) | copy-start | bytes 6148
Sparse Core Ops, SparseCore 0:
  292.4 40.5 all-gather.2
where the time goes:
time: 780 us; the launch traced here: 777 us
  matrix products  609 us (78%)
  waiting for transfers between devices  58.8 us (8%)
  blocking collectives  37.7 us (5%)
  local copies, waits for them, and re-layouts  35.4 us (5%)
  between operations  16.2 us (2%)
  starting transfers between devices  11.5 us (1%)
  other arithmetic  8.27 us (1%)
    dot_general x12, matrix products, product(): jnp.einsum(form, first[1], second[1], precision=HIGHEST)  169 us
    dot_general x12, matrix products, product(): jnp.einsum(form, first[0], second[1], precision=HIGHEST)  155 us
    dot_general x12, matrix products, product(): jnp.einsum(form, first[1], second[0], precision=HIGHEST)  146 us
    dot_general x12, matrix products, product(): jnp.einsum(form, first[0], second[0], precision=HIGHEST)  140 us
    all_gather x1, waiting for transfers between devices, local(): portion = lax.all_gather(returned[None], 'col', axis=0, tiled=True)  40.7 us
    all_to_all x1, blocking collectives, gather_terms(): lax.all_to_all(stacked, ('facet', 'col'), split_axis=0, concat_axis=0, ti...  26.9 us
    all_to_all x1, waiting for transfers between devices, gather_terms(): lax.all_to_all(stacked, ('facet', 'col'), split_axis=0, concat_axis=0, ti...  18.1 us
  transfers between devices with their start and end apart: 2, of which 2 were waited for; matrix products, arithmetic and copies ran while one was open for 0% of the time, Pallas kernels for 0%

commit v1 on v0

v1 whole, which is shorter than its diff:
```python
import math

import jax
import jax.numpy as jnp
from jax import lax
from jax.experimental import pallas as pl
from jax.experimental.pallas import tpu as pltpu
from jax.sharding import PartitionSpec as P

FN = 8192
M = 32
SLOTS = 8
NIMG = 65536
G = 256
FROWS = 128
NF = 16
NC = 8
SLAB = 16
LJ = 256
NI = 32
SHRINK = 0.5
F32 = jnp.float32
MESH = pl.DeviceIdType.MESH


def iota(shape, dim):
    return lax.broadcasted_iota(jnp.int32, shape, dim)


def turns(k, bits, scale):
    n = 1 << bits
    k = k & (n - 1)
    q = (k + n // 8) >> (bits - 2)
    x = (k - (q << (bits - 2))).astype(F32) * (2.0 * math.pi / n)
    y = x * x
    s = x * (1.0 + y * (-1.0 / 6 + y * (1.0 / 120 + y * (-1.0 / 5040 + y * (1.0 / 362880)))))
    c = 1.0 + y * (-0.5 + y * (1.0 / 24 + y * (-1.0 / 720 + y * (1.0 / 40320 + y * (-1.0 / 3628800)))))
    swap = (q & 1) == 1
    cc = jnp.where(swap, s, c) * scale
    ss = jnp.where(swap, c, s) * scale
    return (
        jnp.where(((q + 1) & 2) != 0, -cc, cc),
        jnp.where((q & 2) != 0, -ss, ss),
    )


def dot(a, b):
    return lax.dot_general(
        a, b, (((1,), (0,)), ((), ())),
        precision=lax.Precision.HIGH, preferred_element_type=F32,
    )


def kernel(
    offs, rows, cols, sky_h, obs_h, wts_h,
    new_h, pred_h,
    sky, obs, wts, new, pred,
    bm, bt, at, vt, vb, wz, wt, tf, pt, pk, zs, tt, rr, uu,
    send1, recv1, send2, recv2, send3, recv3, send4, recv4, send5, recv5, send6, recv6,
    ssem, rsem, isem, osem,
):
    f = lax.axis_index("facet")
    c = lax.axis_index("col")

    loads = [
        pltpu.make_async_copy(sky_h, sky, isem.at[0]),
        pltpu.make_async_copy(obs_h, obs, isem.at[1]),
        pltpu.make_async_copy(wts_h, wts, isem.at[2]),
    ]
    for cp in loads:
        cp.start()

    barrier = pltpu.get_barrier_semaphore()
    for k in range(1, NF):
        pl.semaphore_signal(barrier, inc=1, device_id={"facet": lax.rem(f + k, NF)}, device_id_type=MESH)
    for k in range(1, NC):
        pl.semaphore_signal(barrier, inc=1, device_id={"col": lax.rem(c + k, NC)}, device_id_type=MESH)

    def begin(phase, send, recv, axis, n, me):
        copies = []
        for k in range(1, n):
            peer = lax.rem(me + k, n)
            cp = pltpu.make_async_remote_copy(
                src_ref=send.at[peer],
                dst_ref=recv.at[me],
                send_sem=ssem.at[phase, k],
                recv_sem=rsem.at[phase, k],
                device_id={axis: peer},
                device_id_type=MESH,
            )
            cp.start()
            copies.append(cp)
        recv[me] = send[me]
        return copies

    s_me = offs[f, 0]
    t_me = offs[f, 1]
    lane = iota((1, 128), 1)
    low = lane < 64
    part = (lane >> 5) & 1

    l256 = iota((1, LJ), 1)
    cv = 8 * (l256 & 31)
    for b in range(NC):
        cv = cv + jnp.where((l256 >> 5) == b, cols[b], 0)
    bc, bs = turns(iota((LJ, LJ), 0) * cv, 16, 1.0)
    bm[0:256, 0:256] = bc
    bm[0:256, 256:512] = -bs
    bm[256:512, 0:256] = bs
    bm[256:512, 256:512] = bc
    ac, as_ = turns((t_me * FN + LJ * iota((NI, LJ), 0)) * cv, 16, 1.0 / math.sqrt(FN))
    at[0] = ac
    at[1] = as_

    def columns_forward(image, send):
        x = [
            jnp.concatenate([image[d, :, LJ * i:LJ * (i + 1)] for i in range(NI)], axis=0)
            for d in range(2)
        ]
        zs[...] = dot(jnp.concatenate(x, axis=1), bm[...])
        re = jnp.zeros((SLAB, LJ), F32)
        im = jnp.zeros((SLAB, LJ), F32)
        for i in range(NI):
            zr = zs[SLAB * i:SLAB * (i + 1), 0:256]
            zi = zs[SLAB * i:SLAB * (i + 1), 256:512]
            wc = at[0, i:i + 1, :]
            ws = at[1, i:i + 1, :]
            re = re + (wc * zr + ws * zi)
            im = im + (wc * zi - ws * zr)
        for g in range(2):
            rot_re = [re[:, 128 * g:128 * g + 128]]
            rot_im = [im[:, 128 * g:128 * g + 128]]
            for m in range(1, 4):
                rot_re.append(pltpu.roll(rot_re[0], 32 * m, 1))
                rot_im.append(pltpu.roll(rot_im[0], 32 * m, 1))
            for k in range(4):
                send[4 * g + k] = jnp.where(
                    low,
                    jnp.where(part == 0, rot_re[(4 - k) % 4], rot_im[(5 - k) % 4]),
                    jnp.where(part == 0, rot_re[(6 - k) % 4], rot_im[(7 - k) % 4]),
                )

    def rows_forward(recv, send):
        x = recv[...].reshape(FROWS, 128)
        y = pltpu.roll(x, 32, 1)
        y = jnp.where(part == 0, y, -y)
        out = dot(vt[...], jnp.concatenate([x, y], axis=0))
        send[...] = jnp.where(low, out[0:256], out[256:512]).reshape(NF, SLAB, 128)

    def model(recv):
        x = recv[...].reshape(256, 128)
        for h in range(2):
            zs[256 * h:256 * (h + 1), :] = dot(x, wz[128 * h:128 * (h + 1), :])
        for h in range(2):
            for a in range(NF):
                r0 = 256 * h + SLAB * a
                zr = zs[r0:r0 + SLAB, 0:256]
                zi = zs[r0:r0 + SLAB, 256:512]
                wc = tf[0, a:a + 1, :]
                ws = tf[1, a:a + 1, :]
                vr = wc * zr + ws * zi
                vi = wc * zi - ws * zr
                tt[r0:r0 + SLAB, 0:256] = vr
                tt[r0:r0 + SLAB, 256:512] = vi
                tt[512 + r0:512 + r0 + SLAB, 0:256] = vi
                tt[512 + r0:512 + r0 + SLAB, 256:512] = -vr
        return dot(pt[...], tt[...])

    loads[0].wait()
    columns_forward(sky, send1)
    pl.semaphore_wait(barrier, NF - 1 + NC - 1)
    sent = begin(0, send1, recv1, "col", NC, c)

    p16 = iota((SLAB, 128), 0)
    r128 = s_me * FN + iota((SLAB, 128), 1)
    vscale = 1.0 / math.sqrt(FROWS)
    for h in range(2):
        for a in range(NF):
            vc, vs = turns(r128 * (rows[a] + 512 * (SLAB * h + p16)), 16, vscale)
            r0 = 256 * h + SLAB * a
            vt[r0:r0 + SLAB, 0:128] = vc
            vt[r0:r0 + SLAB, 128:256] = vs
    for cp in sent:
        cp.wait_recv()
    rows_forward(recv1, send2)
    sent2 = begin(1, send2, recv2, "facet", NF, f)

    c16, s16 = turns(iota((M, G), 0) * iota((M, G), 1), 8, 1.0 / 16)
    zero = jnp.zeros((64, 512), F32)
    for h in range(2):
        r0 = 128 * h + 64 * h
        wz[r0:r0 + 32, 0:256] = c16
        wz[r0:r0 + 32, 256:512] = -s16
        wz[r0 + 32:r0 + 64, 0:256] = s16
        wz[r0 + 32:r0 + 64, 256:512] = c16
        z0 = 128 * h + 64 * (1 - h)
        wz[z0:z0 + 64, :] = zero
    tv = jnp.zeros((NF, G), jnp.int32)
    i16 = iota((NF, G), 0)
    for a in range(NF):
        tv = jnp.where(i16 == a, offs[a, 1], tv)
    tc, ts = turns(tv * iota((NF, G), 1), 3, 1.0)
    tf[0] = tc
    tf[1] = ts
    l512 = iota((1, 512), 1)
    place = (l512 & 15) + SLAB * (l512 >> 8)
    for a in range(NF):
        place = place + jnp.where(((l512 >> 4) & 15) == a, offs[a, 0] * M, 0)
    pc, ps_ = turns(iota((G, 512), 0) * place, 8, 1.0 / 16)
    pt[:, 0:512] = pc
    pt[:, 512:1024] = ps_
    u256 = iota((SLAB, G), 1)
    q16 = iota((SLAB, G), 0)
    for h in range(2):
        for a in range(NF):
            kc, ks = turns((offs[a, 0] * M + SLAB * h + q16) * u256, 8, 1.0 / 16)
            r0 = 256 * h + SLAB * a
            pk[r0:r0 + SLAB, 0:256] = kc
            pk[r0:r0 + SLAB, 256:512] = ks
    wc_, ws_ = turns(iota((G, 128), 0) * (lane & 31), 8, 1.0 / 16)
    wt[0:256, :] = jnp.where(part == 0, wc_, ws_)
    wt[256:512, :] = jnp.where(part == 0, -ws_, wc_)
    loads[1].wait()
    loads[2].wait()
    for cp in sent2:
        cp.wait_recv()

    first = model(recv2)
    mask = wts[...].astype(F32)
    rre = mask * (obs[0] - first[:, 0:256])
    rim = mask * (obs[1] - first[:, 256:512])
    rr[0:256, 0:256] = rre
    rr[0:256, 256:512] = rim
    rr[256:512, 0:256] = -rim
    rr[256:512, 256:512] = rre
    zs[...] = dot(pk[...], rr[...])
    for h in range(2):
        for a in range(NF):
            r0 = 256 * h + SLAB * a
            zr = zs[r0:r0 + SLAB, 0:256]
            zi = zs[r0:r0 + SLAB, 256:512]
            wc = tf[0, a:a + 1, :]
            ws = tf[1, a:a + 1, :]
            uu[r0:r0 + SLAB, 0:256] = wc * zr - ws * zi
            uu[r0:r0 + SLAB, 256:512] = wc * zi + ws * zr
    out = dot(uu[...], wt[...])
    send3[...] = jnp.where(low, out[0:256], out[256:512]).reshape(NF, SLAB, 128)
    sent3 = begin(2, send3, recv3, "facet", NF, f)

    fl = 512 * (l256 & 15)
    for a in range(NF):
        fl = fl + jnp.where((l256 >> 4) == a, rows[a], 0)
    rcol = s_me * FN + iota((FROWS, LJ), 0)
    for h in range(2):
        vc, vs = turns(rcol * (fl + 512 * SLAB * h), 16, vscale)
        vb[128 * h:128 * h + 128, :] = vc
        vb[256 + 128 * h:256 + 128 * h + 128, :] = vs
    j256 = iota((M, LJ), 1)
    q32 = iota((M, LJ), 0)
    for b in range(NC):
        bc, bs = turns(j256 * (cols[b] + 8 * q32), 16, 1.0)
        bt[32 * b:32 * b + 32, 0:256] = bc
        bt[32 * b:32 * b + 32, 256:512] = bs
        bt[256 + 32 * b:256 + 32 * b + 32, 0:256] = -bs
        bt[256 + 32 * b:256 + 32 * b + 32, 256:512] = bc
    for cp in sent3:
        cp.wait_recv()

    out = dot(vb[...], recv3[...].reshape(256, 128))
    dd = jnp.where(low, out[0:128], out[128:256])
    ee = jnp.where(low, out[256:384], out[384:512])
    dd = dd + pltpu.roll(dd, 64, 1)
    ee = ee + pltpu.roll(ee, 64, 1)
    ee = pltpu.roll(ee, 32, 1)
    send4[...] = (dd + jnp.where(part == 0, -ee, ee)).reshape(NC, SLAB, 128)
    sent4 = begin(3, send4, recv4, "col", NC, c)
    for cp in sent4:
        cp.wait_recv()

    tiles_re = []
    tiles_im = []
    for g in range(2):
        a = [recv4[4 * g + k] for k in range(4)]
        w = [pltpu.roll(v, 32, 1) for v in a]
        tiles_re.append(
            jnp.where(low, jnp.where(part == 0, a[0], w[1]), jnp.where(part == 0, a[2], w[3]))
        )
        tiles_im.append(
            jnp.where(low, jnp.where(part == 0, w[0], a[1]), jnp.where(part == 0, w[2], a[3]))
        )
    sre = jnp.concatenate(tiles_re, axis=1)
    sim = jnp.concatenate(tiles_im, axis=1)
    for i in range(NI):
        wc = at[0, i:i + 1, :]
        ws = at[1, i:i + 1, :]
        uu[SLAB * i:SLAB * (i + 1), 0:256] = sre * wc - sim * ws
        uu[SLAB * i:SLAB * (i + 1), 256:512] = sim * wc + sre * ws
    zs[...] = dot(uu[...], bt[...])
    for i in range(NI):
        ur = sky[0, :, LJ * i:LJ * (i + 1)] + zs[SLAB * i:SLAB * (i + 1), 0:256]
        ui = sky[1, :, LJ * i:LJ * (i + 1)] + zs[SLAB * i:SLAB * (i + 1), 256:512]
        mag = jnp.sqrt(ur * ur + ui * ui)
        ratio = jnp.maximum(mag - SHRINK, 0.0) / jnp.maximum(mag, SHRINK)
        new[0, :, LJ * i:LJ * (i + 1)] = ur * ratio
        new[1, :, LJ * i:LJ * (i + 1)] = ui * ratio
    store_new = pltpu.make_async_copy(new, new_h, osem.at[0])
    store_new.start()

    columns_forward(new, send5)
    sent5 = begin(4, send5, recv5, "col", NC, c)
    for cp in sent5:
        cp.wait_recv()
    rows_forward(recv5, send6)
    sent6 = begin(5, send6, recv6, "facet", NF, f)
    for cp in sent6:
        cp.wait_recv()
    second = model(recv6)
    pred[0] = second[:, 0:256]
    pred[1] = second[:, 256:512]
    store_pred = pltpu.make_async_copy(pred, pred_h, osem.at[1])
    store_pred.start()
    for group in (sent, sent2, sent3, sent4, sent5, sent6):
        for cp in group:
            cp.wait_send()
    store_new.wait()
    store_pred.wait()


def local(sky_image, observed, weights, facet_offsets, subgrid_rows, subgrid_columns):
    smem = pl.BlockSpec(memory_space=pltpu.SMEM)
    hbm = pl.BlockSpec(memory_space=pl.ANY)
    small = pltpu.VMEM((NC, SLAB, 128), F32)
    large = pltpu.VMEM((NF, SLAB, 128), F32)
    square = pltpu.VMEM((512, 512), F32)
    return pl.pallas_call(
        kernel,
        out_shape=(
            jax.ShapeDtypeStruct((2, SLAB, FN), F32),
            jax.ShapeDtypeStruct((2, G, G), F32),
        ),
        in_specs=[smem, smem, smem, hbm, hbm, hbm],
        out_specs=(hbm, hbm),
        scratch_shapes=[
            pltpu.VMEM((2, SLAB, FN), F32),
            pltpu.VMEM((2, G, G), F32),
            pltpu.VMEM((G, G), jnp.int32),
            pltpu.VMEM((2, SLAB, FN), F32),
            pltpu.VMEM((2, G, G), F32),
            square,
            square,
            pltpu.VMEM((2, NI, LJ), F32),
            pltpu.VMEM((512, 256), F32),
            pltpu.VMEM((512, 256), F32),
            pltpu.VMEM((256, 512), F32),
            pltpu.VMEM((512, 128), F32),
            pltpu.VMEM((2, NF, G), F32),
            pltpu.VMEM((256, 1024), F32),
            square,
            square,
            pltpu.VMEM((1024, 512), F32),
            square,
            square,
            small, small, large, large, large, large, small, small, small, small, large, large,
            pltpu.SemaphoreType.DMA((6, NF)),
            pltpu.SemaphoreType.DMA((6, NF)),
            pltpu.SemaphoreType.DMA((3,)),
            pltpu.SemaphoreType.DMA((2,)),
        ],
        compiler_params=pltpu.CompilerParams(
            collective_id=0, has_side_effects=True, vmem_limit_bytes=40 * 1024 * 1024
        ),
        name="imaging",
    )(facet_offsets, subgrid_rows, subgrid_columns, sky_image, observed, weights)


def solution(mesh):
    return jax.shard_map(
        local,
        mesh=mesh,
        in_specs=(
            P(None, ("facet", "col"), None),
            P(None, "facet", "col"),
            P("facet", "col"),
            P(),
            P(),
            P(),
        ),
        out_specs=(P(None, ("facet", "col"), None), P(None, "facet", "col")),
        check_vma=False,
    )
```

time: 780 us -> 53.6 us (0.07)
  matrix products: 609 us -> 0 us
  waiting for transfers between devices: 58.8 us -> 0 us
  Pallas kernels: 0 us -> 47 us
  blocking collectives: 37.7 us -> 0 us
  local copies, waits for them, and re-layouts: 35.4 us -> 5.76 us
  between operations: 16.2 us -> 0.66 us
  starting transfers between devices: 11.5 us -> 0 us
  other arithmetic: 8.27 us -> 0 us
    dot_general x48 -> x0, matrix products: 609 us -> none  [the longest x12 169 us: product(): jnp.einsum(form, first[1], second[1], precision=HIGHEST)]
    pallas_call x0 -> x1, Pallas kernels: none -> 47 us  [local(): pl.pallas_call(kernel, out_shape=(jax.ShapeDtypeStruct((2, SLAB, FN), F32...]
    all_gather x1 -> x0, waiting for transfers between devices: 40.7 us -> none  [local(): portion = lax.all_gather(returned[None], 'col', axis=0, tiled=True)]
    all_to_all x2 -> x0, blocking collectives: 37.7 us -> none  [the longest x1 26.9 us: gather_terms(): lax.all_to_all(stacked, ('facet', 'col'), split_axis=0, concat_axis=0, ti...]
    all_to_all x1 -> x0, waiting for transfers between devices: 18.1 us -> none  [gather_terms(): lax.all_to_all(stacked, ('facet', 'col'), split_axis=0, concat_axis=0, ti...]
    reshape x7 -> x0, local copies, waits for them, and re-layouts: 13.1 us -> none  [the longest x4 10.1 us: gather_terms(): stacked = partials(facet_slab, width).transpose(1, 3, 0, 2, 4).reshape(fa...]
    all_to_all x1 -> x0, starting transfers between devices: 11.5 us -> none  [gather_terms(): lax.all_to_all(stacked, ('facet', 'col'), split_axis=0, concat_axis=0, ti...]
    slice x4 -> x0, local copies, waits for them, and re-layouts: 9.61 us -> none  [the longest x2 5.82 us: local(): matrix[1]]
  transfers between devices with their start and end apart: 2 -> 0, of which waited for: 2 -> 0; matrix products, arithmetic and copies ran while one was open for 0% -> 0% of each run, Pallas kernels for 0% -> 0%
where the time goes in v1:
time: 53.6 us; the launch traced here: 53.4 us
  Pallas kernels  47 us (88%)
  local copies, waits for them, and re-layouts  5.76 us (11%)
  between operations  0.66 us (1%)
    pallas_call x1, Pallas kernels, local(): pl.pallas_call(kernel, out_shape=(jax.ShapeDtypeStruct((2, SLAB, FN), F32...  47 us
    unnamed x13, local copies, waits for them, and re-layouts  5.76 us

profile of v1, /device:TPU:1, one launch (start us, length us, event | category | flops | bytes accessed | tf_op | source)
XLA Modules:
  0.0 53.4 jit_solution(4066096080650461597)
XLA Ops:
  0.6 0.0 copy-start.4
  0.6 0.0 copy-start.3
  0.7 0.8 %copy.8.offs = s32[16,2]{1,0:T(8,128)S(1)} copy(s32[16,2]{0,1:T(2,128)} %param.9) | data formatting | bytes 256 | tf_op args[3]
  1.4 0.0 copy-done.4
  1.4 0.0 copy-done.3
  1.4 0.0 copy-start
  1.4 1.2 %copy-done = f32[2,16,8192]{2,1,0:T(8,128)S(1)} copy-done((f32[2,16,8192]{2,1,0:T(8,128)S(1)}, f32[2,16,8192]{2,1,0:T(8,128)}, u32[]{:S(2)}) %copy-start) | copy-done | bytes 1048600
  2.6 0.0 copy-start.1
  2.7 1.0 %copy-done.1 = f32[2,256,256]{2,1,0:T(8,128)S(1)} copy-done((f32[2,256,256]{2,1,0:T(8,128)S(1)}, f32[2,256,256]{2,1,0:T(8,128)}, u32[]{:S(2)}) %copy-start.1) | copy-done | bytes 524312
  3.7 0.0 copy-start.2
  3.7 0.9 %copy-done.2 = s32[256,256]{1,0:T(8,128)S(1)} copy-done((s32[256,256]{1,0:T(8,128)S(1)}, s32[256,256]{1,0:T(8,128)}, u32[]{:S(2)}) %copy-start.2) | copy-done | bytes 262168
  4.6 47.0 %imaging.1 = (f32[2,16,8192]{2,1,0:T(8,128)S(1)}, f32[2,256,256]{2,1,0:T(8,128)S(1)}) custom-call(s32[16,2]{1,0:T(8,128)S(1)} %copy.8.offs, s32[16]{0:T(128)S(1)} %copy-done.3, s32[8]{0:T(128)S(1)} %copy-done.4, f32[2,16,8192]{2,1,0:T(8,128)S(1)} %copy-done, f32[2,256,256]{2,1,0:T(8,128)S(1)} %copy-done.1, s32[256,256]{1,0:T(8,128)S(1)} %copy-done.2), custom_call_target="tpu_custom_call" | custom-call | tf_op jit(solution)/shard_map/imaging/pallas_call | solution.py:335
  51.6 1.0 %copy.11 = f32[2,16,8192]{2,1,0:T(8,128)} copy(f32[2,16,8192]{2,1,0:T(8,128)S(1)} %get-tuple-element.4) | data formatting | bytes 2097152
  52.6 0.8 %copy.12 = f32[2,256,256]{2,1,0:T(8,128)} copy(f32[2,256,256]{2,1,0:T(8,128)S(1)} %get-tuple-element.5) | data formatting | bytes 1048576
Async XLA Ops:
  0.6 0.8 %copy-start.4 = (s32[8]{0:T(128)S(1)}, s32[8]{0:T(128)}, u32[]{:S(2)}) copy-start(s32[8]{0:T(128)} %cols.1) | copy-start | bytes 100
  0.6 0.8 %copy-start.3 = (s32[16]{0:T(128)S(1)}, s32[16]{0:T(128)}, u32[]{:S(2)}) copy-start(s32[16]{0:T(128)} %rows.1) | copy-start | bytes 196
  1.4 1.2 %copy-start = (f32[2,16,8192]{2,1,0:T(8,128)S(1)}, f32[2,16,8192]{2,1,0:T(8,128)}, u32[]{:S(2)}) copy-start(f32[2,16,8192]{2,1,0:T(8,128)} %sky_h.1) | copy-start | bytes 3145732
  2.6 1.0 %copy-start.1 = (f32[2,256,256]{2,1,0:T(8,128)S(1)}, f32[2,256,256]{2,1,0:T(8,128)}, u32[]{:S(2)}) copy-start(f32[2,256,256]{2,1,0:T(8,128)} %obs_h.1) | copy-start | bytes 1572868
  3.7 0.9 %copy-start.2 = (s32[256,256]{1,0:T(8,128)S(1)}, s32[256,256]{1,0:T(8,128)}, u32[]{:S(2)}) copy-start(s32[256,256]{1,0:T(8,128)} %wts_h.1) | copy-start | bytes 786436

commit v2 on v1

v2 whole, which is shorter than its diff:
```python
import math

import jax
import jax.numpy as jnp
from jax import lax
from jax.experimental import pallas as pl
from jax.experimental.pallas import tpu as pltpu
from jax.sharding import PartitionSpec as P

FN = 8192
M = 32
SLOTS = 8
NIMG = 65536
G = 256
FROWS = 128
NF = 16
NC = 8
SLAB = 16
LJ = 256
NI = 32
SHRINK = 0.5
F32 = jnp.float32
BF16 = jnp.bfloat16
MESH = pl.DeviceIdType.MESH


def iota(shape, dim):
    return lax.broadcasted_iota(jnp.int32, shape, dim)


def turns(k, bits, scale):
    n = 1 << bits
    k = k & (n - 1)
    q = (k + n // 8) >> (bits - 2)
    x = (k - (q << (bits - 2))).astype(F32) * (2.0 * math.pi / n)
    y = x * x
    s = x * (1.0 + y * (-1.0 / 6 + y * (1.0 / 120 + y * (-1.0 / 5040 + y * (1.0 / 362880)))))
    c = 1.0 + y * (-0.5 + y * (1.0 / 24 + y * (-1.0 / 720 + y * (1.0 / 40320 + y * (-1.0 / 3628800)))))
    swap = (q & 1) == 1
    cc = jnp.where(swap, s, c) * scale
    ss = jnp.where(swap, c, s) * scale
    return (
        jnp.where(((q + 1) & 2) != 0, -cc, cc),
        jnp.where((q & 2) != 0, -ss, ss),
    )


def split(x):
    high = x.astype(BF16)
    return high, (x - high.astype(F32)).astype(BF16)


def put_left(ref, rows, start, x):
    high, rest = split(x)
    k = ref.shape[-1] // 3
    n = x.shape[1]
    ref[rows, start:start + n] = high
    ref[rows, k + start:k + start + n] = rest
    ref[rows, 2 * k + start:2 * k + start + n] = high


def put_right(ref, start, columns, x):
    high, rest = split(x)
    k = ref.shape[-2] // 3
    n = x.shape[0]
    ref[start:start + n, columns] = high
    ref[k + start:k + start + n, columns] = high
    ref[2 * k + start:2 * k + start + n, columns] = rest


def right(x):
    high, rest = split(x)
    return jnp.concatenate([high, high, rest], axis=0)


def dot(a, b):
    return lax.dot_general(a, b, (((1,), (0,)), ((), ())), preferred_element_type=F32)


def span(start, size):
    return slice(start, start + size)


ALL = slice(None)
COL_STEPS = ((1, 2), (1, 1), (1, 3), (0, 2), (1, 0), (0, 1), (0, 3))
FACET_STEPS = tuple(
    sorted(
        ((y, x, k) for y in range(4) for x in range(2) for k in range(2) if y + x + k > 0),
        key=lambda d: -(min(d[0], 4 - d[0]) + d[1]),
    )
)


def lanes():
    lane = iota((1, 128), 1)
    return lane < 64, (lane >> 5) & 1


def model(parts, wz, tf, pt, zs, tt):
    low, _ = lanes()
    x = parts[...].reshape(256, 128)
    high = x.astype(BF16).astype(F32)
    rest = x - high
    a = jnp.concatenate(
        [
            jnp.where(low, high, pltpu.roll(rest, 64, 1)),
            jnp.where(low, pltpu.roll(high, 64, 1), rest),
        ],
        axis=0,
    ).astype(BF16)
    zs[...] = dot(jnp.concatenate([a, a], axis=1), wz[...])
    sums = []
    for h in range(2):
        for k in range(NF):
            rows = span(256 * h + SLAB * k, SLAB)
            zr = zs[rows, 0:256]
            zi = zs[rows, 256:512]
            wc = tf[0, k:k + 1, :]
            ws = tf[1, k:k + 1, :]
            put_right(tt.at[h], SLAB * k, span(0, 256), wc * zr + ws * zi)
            put_right(tt.at[h], SLAB * k, span(256, 256), wc * zi - ws * zr)
        g = dot(pt[span(256 * h, 256), :], tt[h])
        sums.append((g[0:128, 0:256] + g[128:256, 256:512], g[0:128, 256:512] - g[128:256, 0:256]))
    (er, ei), (odd_r, odd_i) = sums
    return (er + odd_r, ei + odd_i), (er - odd_r, ei - odd_i)


def finish_kernel(parts, wz, tf, pt, new, new_h, pred_h, pred, zs, tt, sem):
    store_new = pltpu.make_async_copy(new, new_h, sem.at[0])
    store_new.start()
    stores = [store_new]
    for half, values in enumerate(model(parts, wz, tf, pt, zs, tt)):
        for d in range(2):
            rows = span(128 * half, 128)
            pred[d, rows, :] = values[d]
            cp = pltpu.make_async_copy(pred.at[d, rows, :], pred_h.at[d, rows, :], sem.at[1 + 2 * half + d])
            cp.start()
            stores.append(cp)
    for cp in stores:
        cp.wait()


def kernel(
    offs_h, rows_h, cols_h, sky_h, obs_h, wts_h,
    recv6, wz, tf, pt, new,
    offs, rows, cols, sky, obs, wts,
    bm, bt, at, vt, vb, wt, pk, zs, tt, rt, uu,
    send1, recv1, send2, recv2, send3, recv3, send4, recv4, send5, recv5, send6,
    ssem, rsem, isem,
):
    f = lax.axis_index("facet")
    c = lax.axis_index("col")

    loads = [
        pltpu.make_async_copy(src, dst, isem.at[n])
        for n, (src, dst) in enumerate(
            ((cols_h, cols), (offs_h, offs), (rows_h, rows), (sky_h, sky), (obs_h, obs), (wts_h, wts))
        )
    ]
    for cp in loads:
        cp.start()

    fy, fx, fk = lax.div(f, 4), lax.rem(lax.div(f, 2), 2), lax.rem(f, 2)
    cx, cz = lax.div(c, 4), lax.rem(c, 4)
    col_peers = [4 * lax.rem(cx + x, 2) + lax.rem(cz + z, 4) for x, z in COL_STEPS]
    facet_peers = [
        4 * lax.rem(fy + y, 4) + 2 * lax.rem(fx + x, 2) + lax.rem(fk + k, 2) for y, x, k in FACET_STEPS
    ]
    barrier = pltpu.get_barrier_semaphore()
    for peer in facet_peers:
        pl.semaphore_signal(barrier, inc=1, device_id={"facet": peer}, device_id_type=MESH)
    for peer in col_peers:
        pl.semaphore_signal(barrier, inc=1, device_id={"col": peer}, device_id_type=MESH)

    def start(phase, send, recv, axis):
        me, peers = (c, col_peers) if axis == "col" else (f, facet_peers)

        def copy(src, dst, peer):
            return pltpu.make_async_remote_copy(
                src_ref=src, dst_ref=dst, send_sem=ssem.at[phase], recv_sem=rsem.at[phase],
                device_id={axis: peer}, device_id_type=MESH,
            )

        for peer in peers:
            copy(send.at[peer], recv.at[me], peer).start()
        recv[me] = send[me]
        n = len(peers)
        return copy(send.at[pl.ds(0, n)], recv.at[pl.ds(0, n)], peers[0])

    low, part = lanes()
    lane = iota((1, 128), 1)

    def unpack(x):
        y = pltpu.roll(x, 64, 1)
        return jnp.where(low, x, y), jnp.where(low, y, x)

    l256 = iota((1, LJ), 1)
    cv = 8 * (l256 & 31)
    loads[0].wait()
    for b in range(NC):
        cv = cv + jnp.where((l256 >> 5) == b, cols[b], 0)
    bc, bs = turns(iota((LJ, LJ), 0) * cv, 16, 1.0)
    put_right(bm, 0, span(0, 256), bc)
    put_right(bm, 0, span(256, 256), -bs)
    put_right(bm, 256, span(0, 256), bs)
    put_right(bm, 256, span(256, 256), bc)
    loads[1].wait()
    s_me = offs[0, f]
    t_me = offs[1, f]
    ac, as_ = turns((t_me * FN + LJ * iota((NI, LJ), 0)) * cv, 16, 1.0 / math.sqrt(FN))
    at[0] = ac
    at[1] = as_

    def columns_forward(image, send):
        for i in range(NI):
            for d in range(2):
                put_left(uu, span(SLAB * i, SLAB), 256 * d, image[d, :, LJ * i:LJ * (i + 1)])
        zs[...] = dot(uu[...], bm[...])
        re = jnp.zeros((SLAB, LJ), F32)
        im = jnp.zeros((SLAB, LJ), F32)
        for i in range(NI):
            zr = zs[SLAB * i:SLAB * (i + 1), 0:256]
            zi = zs[SLAB * i:SLAB * (i + 1), 256:512]
            wc = at[0, i:i + 1, :]
            ws = at[1, i:i + 1, :]
            re = re + (wc * zr + ws * zi)
            im = im + (wc * zi - ws * zr)
        for g in range(2):
            rot_re = [re[:, 128 * g:128 * g + 128]]
            rot_im = [im[:, 128 * g:128 * g + 128]]
            for m in range(1, 4):
                rot_re.append(pltpu.roll(rot_re[0], 32 * m, 1))
                rot_im.append(pltpu.roll(rot_im[0], 32 * m, 1))
            for k in range(4):
                send[4 * g + k] = jnp.where(
                    low,
                    jnp.where(part == 0, rot_re[(4 - k) % 4][0:8], rot_im[(5 - k) % 4][0:8]),
                    jnp.where(part == 0, rot_re[(6 - k) % 4][8:16], rot_im[(7 - k) % 4][8:16]),
                )

    def rows_forward(recv, send):
        x = jnp.concatenate(unpack(recv[...].reshape(64, 128)), axis=0)
        y = pltpu.roll(x, 32, 1)
        y = jnp.where(part == 0, y, -y)
        out = dot(vt[...], right(jnp.concatenate([x, y], axis=0)))
        send[...] = jnp.where(low, out[0:256], out[256:512]).reshape(NF, SLAB, 128)

    loads[3].wait()
    columns_forward(sky, send1)
    pl.semaphore_wait(barrier, NF - 1 + NC - 1)
    wait1 = start(0, send1, recv1, "col")

    loads[2].wait()
    p16 = iota((SLAB, 128), 0)
    l128 = iota((SLAB, 128), 1)
    r128 = s_me * FN + SLAB * ((l128 >> 3) & 7) + 8 * (l128 >> 6) + (l128 & 7)
    vscale = 1.0 / math.sqrt(FROWS)
    for h in range(2):
        for a in range(NF):
            vc, vs = turns(r128 * (rows[a] + 512 * (2 * p16 + h)), 16, vscale)
            put_left(vt, span(256 * h + SLAB * a, SLAB), 0, vc)
            put_left(vt, span(256 * h + SLAB * a, SLAB), 128, vs)
    wait1.wait_recv()
    rows_forward(recv1, send2)
    wait2 = start(1, send2, recv2, "facet")

    for d in range(0, M, SLAB):
        wc, ws = turns((d + iota((SLAB, G), 0)) * iota((SLAB, G), 1), 8, 1.0 / 16)
        for r0, n, x in ((d, 0, wc), (d, 256, -ws), (M + d, 0, ws), (M + d, 256, wc)):
            high, rest = split(x)
            wz[r0:r0 + SLAB, n:n + 256] = high
            wz[64 + r0:64 + r0 + SLAB, n:n + 256] = high
            wz[128 + r0:128 + r0 + SLAB, n:n + 256] = rest
    wz[192:256, :] = jnp.zeros((64, 512), BF16)
    tv = jnp.zeros((NF, G), jnp.int32)
    i16 = iota((NF, G), 0)
    for a in range(NF):
        tv = jnp.where(i16 == a, offs[1, a], tv)
    tc, ts = turns(tv * iota((NF, G), 1), 3, 1.0)
    tf[0] = tc
    tf[1] = ts
    place = 2 * (l256 & 15)
    for a in range(NF):
        place = place + jnp.where((l256 >> 4) == a, offs[0, a] * M, 0)
    for h in range(2):
        pc, ps_ = turns(iota((128, 256), 0) * (place + h), 8, 1.0 / 16)
        put_left(pt, span(256 * h, 128), 0, pc)
        put_left(pt, span(256 * h + 128, 128), 0, ps_)
    for h in range(2):
        for a in range(NF):
            kc, ks = turns((offs[0, a] * M + h + 2 * p16) * l128, 8, 1.0 / 16)
            put_left(pk, span(256 * h + SLAB * a, SLAB), 0, kc)
            put_left(pk, span(256 * h + SLAB * a, SLAB), 128, ks)
    wc_, ws_ = turns(iota((G, 128), 0) * (lane & 31), 8, 1.0 / 16)
    put_right(wt, 0, ALL, jnp.where(part == 0, wc_, ws_))
    put_right(wt, 256, ALL, jnp.where(part == 0, -ws_, wc_))
    loads[4].wait()
    loads[5].wait()
    wait2.wait_recv()

    resid = []
    for half, (mr, mi) in enumerate(model(recv2, wz, tf, pt, zs, tt)):
        rs = span(128 * half, 128)
        mask = wts[rs, :].astype(F32)
        resid.append((mask * (obs[0, rs, :] - mr), mask * (obs[1, rs, :] - mi)))
    outs = []
    for h in range(2):
        rr, ri = [
            resid[0][d] + resid[1][d] if h == 0 else resid[0][d] - resid[1][d] for d in range(2)
        ]
        put_right(rt.at[h], 0, span(0, 256), rr)
        put_right(rt.at[h], 0, span(256, 256), ri)
        put_right(rt.at[h], 128, span(0, 256), -ri)
        put_right(rt.at[h], 128, span(256, 256), rr)
        zs[span(256 * h, 256), :] = dot(pk[span(256 * h, 256), :], rt[h])
        for a in range(NF):
            zr = zs[span(256 * h + SLAB * a, SLAB), 0:256]
            zi = zs[span(256 * h + SLAB * a, SLAB), 256:512]
            wc = tf[0, a:a + 1, :]
            ws = tf[1, a:a + 1, :]
            put_left(uu, span(256 * h + SLAB * a, SLAB), 0, wc * zr - ws * zi)
            put_left(uu, span(256 * h + SLAB * a, SLAB), 256, wc * zi + ws * zr)
        outs.append(dot(uu[span(256 * h, 256), :], wt[...]))
    send3[...] = jnp.where(low, outs[0], outs[1]).reshape(NF, SLAB, 128)
    wait3 = start(2, send3, recv3, "facet")

    fl = 1024 * (l256 & 15)
    for a in range(NF):
        fl = fl + jnp.where((l256 >> 4) == a, rows[a], 0)
    r0 = iota((FROWS, LJ), 0)
    rcol = s_me * FN + SLAB * ((r0 >> 3) & 7) + 8 * (r0 >> 6) + (r0 & 7)
    for h in range(2):
        vc, vs = turns(rcol * (fl + 512 * h), 16, vscale)
        put_left(vb, span(128 * h, 128), 0, vc)
        put_left(vb, span(256 + 128 * h, 128), 0, vs)
    j256 = iota((M, LJ), 1)
    q32 = iota((M, LJ), 0)
    for b in range(NC):
        bc, bs = turns(j256 * (cols[b] + 8 * q32), 16, 1.0)
        put_right(bt, 32 * b, span(0, 256), bc)
        put_right(bt, 32 * b, span(256, 256), bs)
        put_right(bt, 256 + 32 * b, span(0, 256), -bs)
        put_right(bt, 256 + 32 * b, span(256, 256), bc)
    wait3.wait_recv()

    out = dot(vb[...], right(recv3[...].reshape(256, 128)))
    dd = jnp.where(low, out[0:128], out[128:256])
    ee = jnp.where(low, out[256:384], out[384:512])
    dd = dd + pltpu.roll(dd, 64, 1)
    ee = ee + pltpu.roll(ee, 64, 1)
    ee = pltpu.roll(ee, 32, 1)
    dd = dd + jnp.where(part == 0, -ee, ee)
    send4[...] = jnp.where(low, dd[0:64], dd[64:128]).reshape(NC, 8, 128)
    wait4 = start(3, send4, recv4, "col")
    wait4.wait_recv()

    x4 = jnp.concatenate(unpack(recv4[...].reshape(64, 128)), axis=0)
    y4 = pltpu.roll(x4, 32, 1)
    tiles = []
    for d in range(2):
        halves = []
        for half in range(2):
            row = []
            for g in range(2):
                a = []
                for k in range(4):
                    src = x4 if (k + d) % 2 == 0 else y4
                    r0 = 64 * half + 8 * (4 * g + k)
                    a.append(src[r0:r0 + 8])
                row.append(
                    jnp.where(low, jnp.where(part == 0, a[0], a[1]), jnp.where(part == 0, a[2], a[3]))
                )
            halves.append(jnp.concatenate(row, axis=1))
        tiles.append(jnp.concatenate(halves, axis=0))
    sre, sim = tiles
    for i in range(NI):
        wc = at[0, i:i + 1, :]
        ws = at[1, i:i + 1, :]
        put_left(uu, span(SLAB * i, SLAB), 0, sre * wc - sim * ws)
        put_left(uu, span(SLAB * i, SLAB), 256, sim * wc + sre * ws)
    zs[...] = dot(uu[...], bt[...])
    for i in range(NI):
        ur = sky[0, :, LJ * i:LJ * (i + 1)] + zs[SLAB * i:SLAB * (i + 1), 0:256]
        ui = sky[1, :, LJ * i:LJ * (i + 1)] + zs[SLAB * i:SLAB * (i + 1), 256:512]
        mag = jnp.sqrt(ur * ur + ui * ui)
        ratio = jnp.maximum(mag - SHRINK, 0.0) / jnp.maximum(mag, SHRINK)
        new[0, :, LJ * i:LJ * (i + 1)] = ur * ratio
        new[1, :, LJ * i:LJ * (i + 1)] = ui * ratio

    columns_forward(new, send5)
    wait5 = start(4, send5, recv5, "col")
    wait5.wait_recv()
    rows_forward(recv5, send6)
    wait6 = start(5, send6, recv6, "facet")
    wait6.wait_recv()
    for wait in (wait1, wait2, wait3, wait4, wait5, wait6):
        wait.wait_send()


def local(sky_image, observed, weights, facet_offsets, subgrid_rows, subgrid_columns):
    vmem = pl.BlockSpec(memory_space=pltpu.VMEM)
    hbm = pl.BlockSpec(memory_space=pltpu.HBM)
    small = pltpu.VMEM((NC, 8, 128), F32)
    large = pltpu.VMEM((NF, SLAB, 128), F32)

    def left(rows, columns):
        return pltpu.VMEM((rows, 3 * columns), BF16)

    def right_of(rows, columns):
        return pltpu.VMEM((3 * rows, columns), BF16)

    operands = [
        pltpu.with_memory_space_constraint(x, pltpu.HBM)
        for x in (facet_offsets.T, subgrid_rows, subgrid_columns, sky_image, observed, weights)
    ]
    halfway = pltpu.VMEM((512, 512), F32)
    stack = pltpu.VMEM((2, 768, 512), BF16)
    parts, wz, tf, pt, new = pl.pallas_call(
        kernel,
        out_shape=(
            pltpu.VMEM((NF, SLAB, 128), F32),
            pltpu.VMEM((256, 512), BF16),
            pltpu.VMEM((2, NF, G), F32),
            pltpu.VMEM((512, 768), BF16),
            pltpu.VMEM((2, SLAB, FN), F32),
        ),
        in_specs=[hbm] * 6,
        out_specs=(vmem,) * 5,
        scratch_shapes=[
            pltpu.SMEM((2, NF), jnp.int32),
            pltpu.SMEM((NF,), jnp.int32),
            pltpu.SMEM((NC,), jnp.int32),
            pltpu.VMEM((2, SLAB, FN), F32),
            pltpu.VMEM((2, G, G), F32),
            pltpu.VMEM((G, G), jnp.int32),
            right_of(512, 512),
            right_of(512, 512),
            pltpu.VMEM((2, NI, LJ), F32),
            left(512, 256),
            left(512, 256),
            right_of(512, 128),
            left(512, 256),
            halfway,
            stack,
            stack,
            left(512, 512),
            small, small, large, large, large, large, small, small, small, small, large,
            pltpu.SemaphoreType.DMA((6,)),
            pltpu.SemaphoreType.DMA((6,)),
            pltpu.SemaphoreType.DMA((6,)),
        ],
        compiler_params=pltpu.CompilerParams(
            collective_id=0, has_side_effects=True, vmem_limit_bytes=40 * 1024 * 1024
        ),
        name="imaging",
    )(*operands)
    return pl.pallas_call(
        finish_kernel,
        out_shape=(
            jax.ShapeDtypeStruct((2, SLAB, FN), F32),
            jax.ShapeDtypeStruct((2, G, G), F32),
        ),
        in_specs=[vmem] * 5,
        out_specs=(hbm, hbm),
        scratch_shapes=[
            pltpu.VMEM((2, G, G), F32),
            halfway,
            stack,
            pltpu.SemaphoreType.DMA((5,)),
        ],
        compiler_params=pltpu.CompilerParams(vmem_limit_bytes=32 * 1024 * 1024),
        name="finish",
    )(parts, wz, tf, pt, new)


def solution(mesh):
    return jax.shard_map(
        local,
        mesh=mesh,
        in_specs=(
            P(None, ("facet", "col"), None),
            P(None, "facet", "col"),
            P("facet", "col"),
            P(),
            P(),
            P(),
        ),
        out_specs=(P(None, ("facet", "col"), None), P(None, "facet", "col")),
        check_vma=False,
    )
```

time: 53.6 us -> 43.1 us (0.80)
  local copies, waits for them, and re-layouts: 5.76 us -> 0 us
  Pallas kernels: 47 us -> 42.4 us
    unnamed x13 -> x0, local copies, waits for them, and re-layouts: 5.76 us -> none
    pallas_call x1 -> x2, Pallas kernels: 47 us -> 42.4 us  [the longest x1 40.7 us: local(): pl.pallas_call(kernel, out_shape=(pltpu.VMEM((NF, SLAB, 128), F32), pltpu...]
where the time goes in v2:
time: 43.1 us; the launch traced here: 43 us
  Pallas kernels  42.4 us (98%)
  between operations  0.64 us (1%)
    pallas_call x1, Pallas kernels, local(): pl.pallas_call(kernel, out_shape=(pltpu.VMEM((NF, SLAB, 128), F32), pltpu...  40.7 us
    pallas_call x1, Pallas kernels, local(): pl.pallas_call(finish_kernel, out_shape=(jax.ShapeDtypeStruct((2, SLAB, F...  1.72 us

profile of v2, /device:TPU:1, one launch (start us, length us, event | category | flops | bytes accessed | tf_op | source)
XLA Modules:
  0.0 43.0 jit_solution(6653224703558136213)
XLA Ops:
  0.6 40.7 %imaging.1 = (f32[16,16,128]{2,1,0:T(8,128)S(1)}, bf16[256,512]{1,0:T(8,128)(2,1)S(1)}, f32[2,16,256]{2,1,0:T(8,128)S(1)}, bf16[512,768]{1,0:T(8,128)(2,1)S(1)}, f32[2,16,8192]{2,1,0:T(8,128)S(1)}) custom-call(s32[2,16]{1,0:T(2,128)} %bitcast.1, s32[16]{0:T(128)} %rows_h.1, s32[8]{0:T(128)} %cols_h.1, f32[2,16,8192]{2,1,0:T(8,128)} %sky_h.1, ...), custom_call_target="tpu_custom_call" | custom-call | tf_op jit(solution)/shard_map/imaging/pallas_call | solution.py:418
  41.3 1.7 %finish.1 = (f32[2,16,8192]{2,1,0:T(8,128)}, f32[2,256,256]{2,1,0:T(8,128)}) custom-call(f32[16,16,128]{2,1,0:T(8,128)S(1)} %get-tuple-element.7.parts, bf16[256,512]{1,0:T(8,128)(2,1)S(1)} %get-tuple-element.8.wz, f32[2,16,256]{2,1,0:T(8,128)S(1)} %get-tuple-element.9.tf, bf16[512,768]{1,0:T(8,128)(2,1)S(1)} %get-tuple-element.10.pt, ...), custom_call_target="tpu_custom_call" | custom-call | tf_op jit(solution)/shard_map/finish/pallas_call | solution.py:457

commit v3 on v2

v3 whole, which is shorter than its diff:
```python
import math

import jax
import jax.numpy as jnp
from jax import lax
from jax.experimental import pallas as pl
from jax.experimental.pallas import tpu as pltpu
from jax.sharding import PartitionSpec as P

FN = 8192
M = 32
SLOTS = 8
NIMG = 65536
G = 256
FROWS = 128
NF = 16
NC = 8
SLAB = 16
LJ = 256
NI = 32
SHRINK = 0.5
F32 = jnp.float32
BF16 = jnp.bfloat16
MESH = pl.DeviceIdType.MESH


def iota(shape, dim):
    return lax.broadcasted_iota(jnp.int32, shape, dim)


def turns(k, bits, scale):
    n = 1 << bits
    k = k & (n - 1)
    q = (k + n // 8) >> (bits - 2)
    x = (k - (q << (bits - 2))).astype(F32) * (2.0 * math.pi / n)
    y = x * x
    s = x * (1.0 + y * (-1.0 / 6 + y * (1.0 / 120 + y * (-1.0 / 5040 + y * (1.0 / 362880)))))
    c = 1.0 + y * (-0.5 + y * (1.0 / 24 + y * (-1.0 / 720 + y * (1.0 / 40320 + y * (-1.0 / 3628800)))))
    swap = (q & 1) == 1
    cc = jnp.where(swap, s, c) * scale
    ss = jnp.where(swap, c, s) * scale
    return (
        jnp.where(((q + 1) & 2) != 0, -cc, cc),
        jnp.where((q & 2) != 0, -ss, ss),
    )


def split(x):
    high = x.astype(BF16)
    return high, (x - high.astype(F32)).astype(BF16)


def put_left(ref, rows, start, x):
    high, rest = split(x)
    k = ref.shape[-1] // 3
    n = x.shape[1]
    ref[rows, start:start + n] = high
    ref[rows, k + start:k + start + n] = rest
    ref[rows, 2 * k + start:2 * k + start + n] = high


def put_right(ref, start, columns, x):
    high, rest = split(x)
    k = ref.shape[-2] // 3
    n = x.shape[0]
    ref[start:start + n, columns] = high
    ref[k + start:k + start + n, columns] = high
    ref[2 * k + start:2 * k + start + n, columns] = rest


def right(x):
    high, rest = split(x)
    return jnp.concatenate([high, high, rest], axis=0)


def dot(a, b):
    return lax.dot_general(a, b, (((1,), (0,)), ((), ())), preferred_element_type=F32)


def span(start, size):
    return slice(start, start + size)


ALL = slice(None)
COL_STEPS = ((1, 2), (1, 1), (1, 3), (0, 2), (1, 0), (0, 1), (0, 3), (0, 0))
FACET_STEPS = (
    (2, 1, 0), (2, 1, 1), (2, 0, 0), (2, 0, 1), (1, 1, 0), (1, 1, 1), (3, 1, 0), (3, 1, 1),
    (1, 0, 0), (1, 0, 1), (3, 0, 0), (3, 0, 1), (0, 1, 0), (0, 1, 1), (0, 0, 1), (0, 0, 0),
)
COL_BACK = tuple(COL_STEPS.index((x, -z % 4)) for x, z in COL_STEPS)
FACET_BACK = tuple(FACET_STEPS.index((-y % 4, x, k)) for y, x, k in FACET_STEPS)
FACET_CROSS = tuple(FACET_STEPS.index((y, x, 1 - k)) for y, x, k in FACET_STEPS)
FACET_CROSS_BACK = tuple(FACET_STEPS.index((-y % 4, x, 1 - k)) for y, x, k in FACET_STEPS)
FAR, NEAR = 0, 1


def lanes():
    lane = iota((1, 128), 1)
    return lane < 64, (lane >> 5) & 1


def model_half(group, parts, wz, tf, pt, zs, tt):
    low, _ = lanes()
    x = parts.reshape(128, 128)
    high = x.astype(BF16).astype(F32)
    rest = x - high
    a = jnp.concatenate(
        [
            jnp.where(low, high, pltpu.roll(rest, 64, 1)),
            jnp.where(low, pltpu.roll(high, 64, 1), rest),
        ],
        axis=0,
    ).astype(BF16)
    zs[0:256, :] = dot(jnp.concatenate([a, a], axis=1), wz[...])
    sums = []
    for h in range(2):
        for k in range(8):
            rows = span(128 * h + SLAB * k, SLAB)
            zr = zs[rows, 0:256]
            zi = zs[rows, 256:512]
            wc = tf[0, 8 * group + k:8 * group + k + 1, :]
            ws = tf[1, 8 * group + k:8 * group + k + 1, :]
            put_right(tt.at[h], SLAB * k, span(0, 256), wc * zr + ws * zi)
            put_right(tt.at[h], SLAB * k, span(256, 256), wc * zi - ws * zr)
        sums.append(dot(pt[group, span(256 * h, 256), :], tt[h]))
    return sums


def combine(even, odd):
    (er, ei), (dr, di) = [
        (s[0:128, 0:256] + s[128:256, 256:512], s[0:128, 256:512] - s[128:256, 0:256])
        for s in (even, odd)
    ]
    return (er + dr, ei + di), (er - dr, ei - di)


def finish_kernel(parts, gs, wz, tf, pt, new, new_h, pred_h, pred, zs, tt, sem):
    store_new = pltpu.make_async_copy(new, new_h, sem.at[0])
    store_new.start()
    stores = [store_new]
    sums = model_half(FAR, parts[...], wz, tf, pt, zs, tt)
    for half, values in enumerate(combine(gs[0:256] + sums[0], gs[256:512] + sums[1])):
        for d in range(2):
            rows = span(128 * half, 128)
            pred[d, rows, :] = values[d]
            cp = pltpu.make_async_copy(pred.at[d, rows, :], pred_h.at[d, rows, :], sem.at[1 + 2 * half + d])
            cp.start()
            stores.append(cp)
    for cp in stores:
        cp.wait()


def kernel(
    offs_h, rows_h, cols_h, sky_h, obs_h, wts_h,
    parts, gs, wz, tf, pt, new,
    offs, rows, cols, sky, obs, wts,
    bm, bt, at, vt, vb, wt, pk, zs, tt, rt, uu, ud,
    send1, recv1, send2, recv2, send3, recv3, send4, recv4, send5, recv5, send6, recv6,
    ssem, rsem, isem,
):
    f = lax.axis_index("facet")
    c = lax.axis_index("col")

    loads = [
        pltpu.make_async_copy(src, dst, isem.at[n])
        for n, (src, dst) in enumerate(
            ((cols_h, cols), (offs_h, offs), (rows_h, rows), (sky_h, sky), (obs_h, obs), (wts_h, wts))
        )
    ]
    for cp in loads:
        cp.start()

    fy, fx, fk = lax.div(f, 4), lax.rem(lax.div(f, 2), 2), lax.rem(f, 2)
    cx, cz = lax.div(c, 4), lax.rem(c, 4)
    col_peers = [4 * lax.rem(cx + x, 2) + lax.rem(cz + z, 4) for x, z in COL_STEPS]
    facet_peers = [
        4 * lax.rem(fy + y, 4) + 2 * lax.rem(fx + x, 2) + lax.rem(fk + k, 2) for y, x, k in FACET_STEPS
    ]
    other = 4 * fy + 2 * fx + (1 - fk)
    barrier = pltpu.get_barrier_semaphore()
    for peer in facet_peers[:-1]:
        pl.semaphore_signal(barrier, inc=1, device_id={"facet": peer}, device_id_type=MESH)
    for peer in col_peers[:-1]:
        pl.semaphore_signal(barrier, inc=1, device_id={"facet": other, "col": peer}, device_id_type=MESH)

    def start(phase, group, send, recv, moves, own=None):
        def copy(src, dst, device):
            return pltpu.make_async_remote_copy(
                src_ref=src, dst_ref=dst, send_sem=ssem.at[phase, group], recv_sem=rsem.at[phase, group],
                device_id=device, device_id_type=MESH,
            )

        for block, slot, device in moves:
            copy(send.at[block], recv.at[slot], device).start()
        if own is not None:
            recv[own[1]] = send[own[0]]
        blocks = pl.ds(0, len(moves))
        return copy(send.at[blocks], recv.at[blocks], moves[0][2])

    def over_columns(phase, group, send, recv, cross=True):
        ks = range(4 * group, 4 * group + 4)
        if cross:
            moves = [(k, COL_BACK[k], {"facet": other, "col": col_peers[k]}) for k in ks]
            return start(phase, group, send, recv, moves)
        moves = [(k, COL_BACK[k], {"col": col_peers[k]}) for k in ks if k < NC - 1]
        return start(phase, group, send, recv, moves, (NC - 1, NC - 1) if group == NEAR else None)

    def to_subgrids(phase, group, send, recv, cross=True):
        back = FACET_CROSS_BACK if cross else FACET_BACK
        ks = range(8 * group, 8 * group + 8)
        moves = [(k, back[k], {"facet": facet_peers[k]}) for k in ks if k < NF - 1]
        return start(phase, group, send, recv, moves, (NF - 1, back[NF - 1]) if group == NEAR else None)

    def to_facets(phase, group, send, recv):
        moves, own = [], None
        for k in range(8 * group, 8 * group + 8):
            if FACET_CROSS[k] < NF - 1:
                moves.append((k, FACET_CROSS_BACK[k], {"facet": facet_peers[FACET_CROSS[k]]}))
            else:
                own = (k, FACET_CROSS_BACK[k])
        return start(phase, group, send, recv, moves, own)

    low, part = lanes()
    lane = iota((1, 128), 1)

    def unpack(x):
        y = pltpu.roll(x, 64, 1)
        return jnp.where(low, x, y), jnp.where(low, y, x)

    l256 = iota((1, LJ), 1)
    cv = 8 * (l256 & 31)
    loads[0].wait()
    for b in range(NC):
        cv = cv + jnp.where((l256 >> 5) == b, cols[col_peers[b]], 0)
    steps = iota((SLAB, LJ), 0)
    c1, s1 = turns((SLAB * steps) * cv, 16, 1.0)
    c0, s0 = turns(steps * cv, 16, 1.0)
    for k in range(SLAB):
        bc = c1[k:k + 1] * c0 - s1[k:k + 1] * s0
        bs = s1[k:k + 1] * c0 + c1[k:k + 1] * s0
        put_right(bm, SLAB * k, span(0, 256), bc)
        put_right(bm, SLAB * k, span(256, 256), -bs)
        put_right(bm, 256 + SLAB * k, span(0, 256), bs)
        put_right(bm, 256 + SLAB * k, span(256, 256), bc)
    loads[1].wait()
    s_me = offs[0, other]
    t_me = offs[1, f]
    ac, as_ = turns((t_me * FN + LJ * iota((NI, LJ), 0)) * cv, 16, 1.0 / math.sqrt(FN))
    at[0] = ac
    at[1] = as_

    def columns_forward(image, send, launch):
        for i in range(NI):
            for d in range(2):
                put_left(uu, span(SLAB * i, SLAB), 256 * d, image[d, :, LJ * i:LJ * (i + 1)])
        zs[...] = dot(uu[...], bm[...])
        re = jnp.zeros((SLAB, LJ), F32)
        im = jnp.zeros((SLAB, LJ), F32)
        for i in range(NI):
            zr = zs[span(SLAB * i, SLAB), 0:256]
            zi = zs[span(SLAB * i, SLAB), 256:512]
            wc = at[0, i:i + 1, :]
            ws = at[1, i:i + 1, :]
            re = re + (wc * zr + ws * zi)
            im = im + (wc * zi - ws * zr)
        for g in range(2):
            rot_re = [re[:, span(128 * g, 128)]]
            rot_im = [im[:, span(128 * g, 128)]]
            for m in range(1, 4):
                rot_re.append(pltpu.roll(rot_re[0], 32 * m, 1))
                rot_im.append(pltpu.roll(rot_im[0], 32 * m, 1))
            for k in range(4):
                send[4 * g + k] = jnp.where(
                    low,
                    jnp.where(part == 0, rot_re[(4 - k) % 4][0:8], rot_im[(5 - k) % 4][0:8]),
                    jnp.where(part == 0, rot_re[(6 - k) % 4][8:16], rot_im[(7 - k) % 4][8:16]),
                )
            launch(g)

    def row_products(vt, group, recv, targets):
        x = jnp.concatenate(unpack(recv[4 * group:4 * group + 4].reshape(32, 128)), axis=0)
        y = pltpu.roll(x, 32, 1)
        y = jnp.where(part == 0, y, -y)
        return dot(vt[group, targets, :], right(jnp.concatenate([x, y], axis=0)))

    def rows_forward(vt, waits, recv, phase, send, into, cross=True):
        waits[NEAR].wait_recv()
        near = row_products(vt, NEAR, recv, ALL)
        zs[:, 0:128] = near
        waits[FAR].wait_recv()
        later = []
        for g in range(2):
            out = zs[span(256 * g, 256), 0:128] + row_products(vt, FAR, recv, span(256 * g, 256))
            send[8 * g:8 * g + 8] = jnp.where(low, out[0:128], out[128:256]).reshape(8, SLAB, 128)
            later.append(to_subgrids(phase, g, send, into, cross))
        return later

    loads[3].wait()
    wait1 = []

    def launch1(g):
        if g == FAR:
            pl.semaphore_wait(barrier, NF - 1 + NC - 1)
        wait1.append(over_columns(0, g, send1, recv1))

    columns_forward(sky, send1, launch1)

    loads[2].wait()

    p16 = iota((SLAB, 128), 0)
    l128 = iota((SLAB, 128), 1)
    vscale = 1.0 / math.sqrt(FROWS)
    lane1 = lane & 63
    for g in range(2):
        slab = jnp.zeros((1, 128), jnp.int32)
        for k in range(4):
            slab = jnp.where(((lane1 >> 3) & 3) == k, col_peers[4 * g + k], slab)
        rlane = s_me * FN + SLAB * slab + 8 * (lane1 >> 5) + (lane1 & 7)
        for a in range(NF):
            for h in range(2):
                vc, vs = turns(rlane * (rows[facet_peers[a]] + 512 * (2 * p16 + h)), 16, vscale)
                r0 = 256 * (a // 8) + 128 * h + SLAB * (a % 8)
                put_left(vt.at[g], span(r0, SLAB), 0, jnp.where(low, vc, vs))
    wait2 = rows_forward(vt, wait1, recv1, 1, send2, recv2)

    for d in range(0, M, SLAB):
        wc, ws = turns((d + iota((SLAB, G), 0)) * iota((SLAB, G), 1), 8, 1.0 / 16)
        for r0, n, x in ((d, 0, wc), (d, 256, -ws), (M + d, 0, ws), (M + d, 256, wc)):
            high, rest = split(x)
            wz[r0:r0 + SLAB, n:n + 256] = high
            wz[64 + r0:64 + r0 + SLAB, n:n + 256] = high
            wz[128 + r0:128 + r0 + SLAB, n:n + 256] = rest
    wz[192:256, :] = jnp.zeros((64, 512), BF16)
    tv = jnp.zeros((NF, G), jnp.int32)
    i16 = iota((NF, G), 0)
    for a in range(NF):
        tv = jnp.where(i16 == a, offs[1, facet_peers[a]], tv)
    tc, ts = turns(tv * iota((NF, G), 1), 3, 1.0)
    tf[0] = tc
    tf[1] = ts
    for g in range(2):
        place = 2 * (lane & 15)
        for k in range(8):
            place = place + jnp.where((lane >> 4) == k, offs[0, facet_peers[8 * g + k]] * M, 0)
        for h in range(2):
            pc, ps_ = turns(iota((128, 128), 0) * (place + h), 8, 1.0 / 16)
            put_left(pt.at[g], span(256 * h, 128), 0, pc)
            put_left(pt.at[g], span(256 * h + 128, 128), 0, ps_)
    for h in range(2):
        for a in range(NF):
            kc, ks = turns((offs[0, facet_peers[a]] * M + h + 2 * p16) * l128, 8, 1.0 / 16)
            put_left(pk, span(256 * h + SLAB * a, SLAB), 0, kc)
            put_left(pk, span(256 * h + SLAB * a, SLAB), 128, ks)
    wc_, ws_ = turns(iota((G, 128), 0) * (lane & 31), 8, 1.0 / 16)
    put_right(wt, 0, ALL, jnp.where(part == 0, wc_, ws_))
    put_right(wt, 256, ALL, jnp.where(part == 0, -ws_, wc_))
    wait2[NEAR].wait_recv()
    for h, x in enumerate(model_half(NEAR, recv2[8:16], wz, tf, pt, zs, tt)):
        gs[span(256 * h, 256), :] = x
    loads[4].wait()
    loads[5].wait()
    wait2[FAR].wait_recv()

    sums = model_half(FAR, recv2[0:8], wz, tf, pt, zs, tt)
    resid = []
    for half, (mr, mi) in enumerate(combine(gs[0:256] + sums[0], gs[256:512] + sums[1])):
        rs = span(128 * half, 128)
        mask = wts[rs, :].astype(F32)
        resid.append((mask * (obs[0, rs, :] - mr), mask * (obs[1, rs, :] - mi)))
    for h in range(2):
        rr, ri = [
            resid[0][d] + resid[1][d] if h == 0 else resid[0][d] - resid[1][d] for d in range(2)
        ]
        put_right(rt.at[h], 0, span(0, 256), rr)
        put_right(rt.at[h], 0, span(256, 256), ri)
        put_right(rt.at[h], 128, span(0, 256), -ri)
        put_right(rt.at[h], 128, span(256, 256), rr)
        zs[span(256 * h, 256), :] = dot(pk[span(256 * h, 256), :], rt[h])
    wait3 = []
    for g in range(2):
        for h in range(2):
            for k in range(8):
                src = span(256 * h + 128 * g + SLAB * k, SLAB)
                dst = span(256 * g + 128 * h + SLAB * k, SLAB)
                zr = zs[src, 0:256]
                zi = zs[src, 256:512]
                wc = tf[0, 8 * g + k:8 * g + k + 1, :]
                ws = tf[1, 8 * g + k:8 * g + k + 1, :]
                put_left(uu, dst, 0, wc * zr - ws * zi)
                put_left(uu, dst, 256, wc * zi + ws * zr)
        out = dot(uu[span(256 * g, 256), :], wt[...])
        send3[8 * g:8 * g + 8] = jnp.where(low, out[0:128], out[128:256]).reshape(8, SLAB, 128)
        wait3.append(to_facets(2, g, send3, recv3))

    r0 = iota((FROWS, 128), 0)
    slab = jnp.zeros((FROWS, 128), jnp.int32)
    for k in range(NC):
        slab = jnp.where(((r0 >> 3) & 7) == k, col_peers[k], slab)
    rcol = s_me * FN + SLAB * slab + 8 * (r0 >> 6) + (r0 & 7)
    for g in range(2):
        fl = 1024 * (lane & 15)
        for k in range(8):
            fl = fl + jnp.where((lane >> 4) == k, rows[facet_peers[8 * g + k]], 0)
        for h in range(2):
            vc, vs = turns(rcol * (fl + 512 * h), 16, vscale)
            put_left(vb.at[g], span(128 * h, 128), 0, vc)
            put_left(vb.at[g], span(256 + 128 * h, 128), 0, vs)
    j256 = iota((M, LJ), 1)
    q32 = iota((M, LJ), 0)
    for b in range(NC):
        bc, bs = turns(j256 * (cols[col_peers[b]] + 8 * q32), 16, 1.0)
        half = bt.at[b // 4]
        r1 = 32 * (b % 4)
        put_right(half, r1, span(0, 256), bc)
        put_right(half, r1, span(256, 256), bs)
        put_right(half, 128 + r1, span(0, 256), -bs)
        put_right(half, 128 + r1, span(256, 256), bc)

    wait3[NEAR].wait_recv()
    zs[:, 0:128] = dot(vb[NEAR], right(recv3[8:16].reshape(128, 128)))
    wait3[FAR].wait_recv()
    out = zs[:, 0:128] + dot(vb[FAR], right(recv3[0:8].reshape(128, 128)))
    dd = jnp.where(low, out[0:128], out[128:256])
    ee = jnp.where(low, out[256:384], out[384:512])
    dd = dd + pltpu.roll(dd, 64, 1)
    ee = ee + pltpu.roll(ee, 64, 1)
    ee = pltpu.roll(ee, 32, 1)
    dd = dd + jnp.where(part == 0, -ee, ee)
    send4[...] = jnp.where(low, dd[0:64], dd[64:128]).reshape(NC, 8, 128)
    wait4 = [over_columns(3, g, send4, recv4) for g in range(2)]

    def columns_back(g):
        x4 = jnp.concatenate(unpack(recv4[4 * g:4 * g + 4].reshape(32, 128)), axis=0)
        y4 = pltpu.roll(x4, 32, 1)
        tiles = []
        for d in range(2):
            halves = []
            for half in range(2):
                a = []
                for k in range(4):
                    src = x4 if (k + d) % 2 == 0 else y4
                    a.append(src[32 * half + 8 * k:32 * half + 8 * k + 8])
                halves.append(
                    jnp.where(low, jnp.where(part == 0, a[0], a[1]), jnp.where(part == 0, a[2], a[3]))
                )
            tiles.append(jnp.concatenate(halves, axis=0))
        sre, sim = tiles
        for i in range(NI):
            wc = at[0, i:i + 1, span(128 * g, 128)]
            ws = at[1, i:i + 1, span(128 * g, 128)]
            put_left(ud, span(SLAB * i, SLAB), 0, sre * wc - sim * ws)
            put_left(ud, span(SLAB * i, SLAB), 128, sim * wc + sre * ws)
        return dot(ud[...], bt[g])

    wait4[NEAR].wait_recv()
    near = columns_back(NEAR)
    for i in range(NI):
        rs = span(SLAB * i, SLAB)
        for d in range(2):
            new[d, :, LJ * i:LJ * (i + 1)] = (
                sky[d, :, LJ * i:LJ * (i + 1)] + near[rs, span(256 * d, 256)]
            )
    wait4[FAR].wait_recv()
    zs[...] = columns_back(FAR)
    for i in range(NI):
        rs = span(SLAB * i, SLAB)
        ur = new[0, :, LJ * i:LJ * (i + 1)] + zs[rs, 0:256]
        ui = new[1, :, LJ * i:LJ * (i + 1)] + zs[rs, 256:512]
        mag = jnp.sqrt(ur * ur + ui * ui)
        ratio = jnp.maximum(mag - SHRINK, 0.0) / jnp.maximum(mag, SHRINK)
        new[0, :, LJ * i:LJ * (i + 1)] = ur * ratio
        new[1, :, LJ * i:LJ * (i + 1)] = ui * ratio

    wait5 = []
    columns_forward(new, send5, lambda g: wait5.append(over_columns(4, g, send5, recv5)))
    wait6 = rows_forward(vt, wait5, recv5, 5, send6, recv6)
    wait6[NEAR].wait_recv()
    for h, x in enumerate(model_half(NEAR, recv6[8:16], wz, tf, pt, zs, tt)):
        gs[span(256 * h, 256), :] = x
    wait6[FAR].wait_recv()
    parts[...] = recv6[0:8]
    for group in (wait1, wait2, wait3, wait4, wait5, wait6):
        for wait in group:
            wait.wait_send()


def local(sky_image, observed, weights, facet_offsets, subgrid_rows, subgrid_columns):
    vmem = pl.BlockSpec(memory_space=pltpu.VMEM)
    hbm = pl.BlockSpec(memory_space=pltpu.HBM)
    small = pltpu.VMEM((NC, 8, 128), F32)
    large = pltpu.VMEM((NF, SLAB, 128), F32)

    def left(rows, columns, *lead):
        return pltpu.VMEM((*lead, rows, 3 * columns), BF16)

    def right_of(rows, columns, *lead):
        return pltpu.VMEM((*lead, 3 * rows, columns), BF16)

    operands = [
        pltpu.with_memory_space_constraint(x, pltpu.HBM)
        for x in (facet_offsets.T, subgrid_rows, subgrid_columns, sky_image, observed, weights)
    ]
    halfway = pltpu.VMEM((512, 512), F32)
    parts, gs, wz, tf, pt, new = pl.pallas_call(
        kernel,
        out_shape=(
            pltpu.VMEM((8, SLAB, 128), F32),
            pltpu.VMEM((512, 512), F32),
            pltpu.VMEM((256, 512), BF16),
            pltpu.VMEM((2, NF, G), F32),
            left(512, 128, 2),
            pltpu.VMEM((2, SLAB, FN), F32),
        ),
        in_specs=[hbm] * 6,
        out_specs=(vmem,) * 6,
        scratch_shapes=[
            pltpu.SMEM((2, NF), jnp.int32),
            pltpu.SMEM((NF,), jnp.int32),
            pltpu.SMEM((NC,), jnp.int32),
            pltpu.VMEM((2, SLAB, FN), F32),
            pltpu.VMEM((2, G, G), F32),
            pltpu.VMEM((G, G), jnp.int32),
            right_of(512, 512),
            right_of(256, 512, 2),
            pltpu.VMEM((2, NI, LJ), F32),
            left(512, 128, 2),
            left(512, 128, 2),
            right_of(512, 128),
            left(512, 256),
            halfway,
            right_of(128, 512, 2),
            right_of(256, 512, 2),
            left(512, 512),
            left(512, 256),
            small, small, large, large, large, large, small, small, small, small, large, large,
            pltpu.SemaphoreType.DMA((6, 2)),
            pltpu.SemaphoreType.DMA((6, 2)),
            pltpu.SemaphoreType.DMA((6,)),
        ],
        compiler_params=pltpu.CompilerParams(
            collective_id=0, has_side_effects=True, vmem_limit_bytes=40 * 1024 * 1024
        ),
        name="imaging",
    )(*operands)
    return pl.pallas_call(
        finish_kernel,
        out_shape=(
            jax.ShapeDtypeStruct((2, SLAB, FN), F32),
            jax.ShapeDtypeStruct((2, G, G), F32),
        ),
        in_specs=[vmem] * 6,
        out_specs=(hbm, hbm),
        scratch_shapes=[
            pltpu.VMEM((2, G, G), F32),
            halfway,
            right_of(128, 512, 2),
            pltpu.SemaphoreType.DMA((5,)),
        ],
        compiler_params=pltpu.CompilerParams(vmem_limit_bytes=32 * 1024 * 1024),
        name="finish",
    )(parts, gs, wz, tf, pt, new)


def solution(mesh):
    return jax.shard_map(
        local,
        mesh=mesh,
        in_specs=(
            P(None, ("facet", "col"), None),
            P(None, "facet", "col"),
            P("facet", "col"),
            P(),
            P(),
            P(),
        ),
        out_specs=(P(None, ("facet", "col"), None), P(None, "facet", "col")),
        check_vma=False,
    )
```

time: 43.1 us -> 41.8 us (0.970)
  Pallas kernels: 42.4 us -> 41 us
    pallas_call x1, Pallas kernels: 40.7 us -> 39.5 us  [local(): pl.pallas_call(kernel, out_shape=(pltpu.VMEM((8, SLAB, 128), F32), pltpu....]
where the time goes in v3:
time: 41.8 us; the launch traced here: 41.7 us
  Pallas kernels  41 us (98%)
  between operations  0.64 us (2%)
    pallas_call x1, Pallas kernels, local(): pl.pallas_call(kernel, out_shape=(pltpu.VMEM((8, SLAB, 128), F32), pltpu....  39.5 us
    pallas_call x1, Pallas kernels, local(): pl.pallas_call(finish_kernel, out_shape=(jax.ShapeDtypeStruct((2, SLAB, F...  1.52 us

profile of v3, /device:TPU:1, one launch (start us, length us, event | category | flops | bytes accessed | tf_op | source)
XLA Modules:
  0.0 41.7 jit_solution(17464848389332863200)
XLA Ops:
  0.6 39.5 %imaging.1 = (f32[8,16,128]{2,1,0:T(8,128)S(1)}, f32[512,512]{1,0:T(8,128)S(1)}, bf16[256,512]{1,0:T(8,128)(2,1)S(1)}, f32[2,16,256]{2,1,0:T(8,128)S(1)}, bf16[2...) custom-call(s32[2,16]{1,0:T(2,128)} %bitcast.1, s32[16]{0:T(128)} %rows_h.1, s32[8]{0:T(128)} %cols_h.1, ...), custom_call_target="tpu_custom_call" | custom-call | tf_op jit(solution)/shard_map/imaging/pallas_call | solution.py:504
  40.2 1.5 %finish.1 = (f32[2,16,8192]{2,1,0:T(8,128)}, f32[2,256,256]{2,1,0:T(8,128)}) custom-call(f32[8,16,128]{2,1,0:T(8,128)S(1)} %get-tuple-element.8.parts, f32[512,512]{1,0:T(8,128)S(1)} %get-tuple-element.9.gs, bf16[256,512]{1,0:T(8,128)(2,1)S(1)} %get-tuple-element.10.wz, f32[2,16,256]{2,1,0:T(8,128)S(1)} %get-tuple-element.11.tf, ...), custom_call_target="tpu_custom_call" | custom-call | tf_op jit(solution)/shard_map/finish/pallas_call | solution.py:545

commit v4 on v3

--- a/solution.py
+++ b/solution.py
@@ -52,11 +52,10 @@
 
 def put_left(ref, rows, start, x):
     high, rest = split(x)
-    k = ref.shape[-1] // 3
+    k = ref.shape[-1] // 2
     n = x.shape[1]
     ref[rows, start:start + n] = high
     ref[rows, k + start:k + start + n] = rest
-    ref[rows, 2 * k + start:2 * k + start + n] = high
 
 
 def put_right(ref, start, columns, x):
@@ -77,6 +76,11 @@
     return lax.dot_general(a, b, (((1,), (0,)), ((), ())), preferred_element_type=F32)
 
 
+def dot3(a, b):
+    k = a.shape[1]
+    return dot(a, b[0:k]) + dot(a[:, 0:k // 2], b[k:k + k // 2])
+
+
 def span(start, size):
     return slice(start, start + size)
 
@@ -88,7 +92,6 @@
     (1, 0, 0), (1, 0, 1), (3, 0, 0), (3, 0, 1), (0, 1, 0), (0, 1, 1), (0, 0, 1), (0, 0, 0),
 )
 COL_BACK = tuple(COL_STEPS.index((x, -z % 4)) for x, z in COL_STEPS)
-FACET_BACK = tuple(FACET_STEPS.index((-y % 4, x, k)) for y, x, k in FACET_STEPS)
 FACET_CROSS = tuple(FACET_STEPS.index((y, x, 1 - k)) for y, x, k in FACET_STEPS)
 FACET_CROSS_BACK = tuple(FACET_STEPS.index((-y % 4, x, 1 - k)) for y, x, k in FACET_STEPS)
 FAR, NEAR = 0, 1
@@ -122,7 +125,7 @@
             ws = tf[1, 8 * group + k:8 * group + k + 1, :]
             put_right(tt.at[h], SLAB * k, span(0, 256), wc * zr + ws * zi)
             put_right(tt.at[h], SLAB * k, span(256, 256), wc * zi - ws * zr)
-        sums.append(dot(pt[group, span(256 * h, 256), :], tt[h]))
+        sums.append(dot3(pt[group, span(256 * h, 256), :], tt[h]))
     return sums
 
 
@@ -197,19 +200,20 @@
         blocks = pl.ds(0, len(moves))
         return copy(send.at[blocks], recv.at[blocks], moves[0][2])
 
-    def over_columns(phase, group, send, recv, cross=True):
-        ks = range(4 * group, 4 * group + 4)
-        if cross:
-            moves = [(k, COL_BACK[k], {"facet": other, "col": col_peers[k]}) for k in ks]
-            return start(phase, group, send, recv, moves)
-        moves = [(k, COL_BACK[k], {"col": col_peers[k]}) for k in ks if k < NC - 1]
-        return start(phase, group, send, recv, moves, (NC - 1, NC - 1) if group == NEAR else None)
-
-    def to_subgrids(phase, group, send, recv, cross=True):
-        back = FACET_CROSS_BACK if cross else FACET_BACK
-        ks = range(8 * group, 8 * group + 8)
-        moves = [(k, back[k], {"facet": facet_peers[k]}) for k in ks if k < NF - 1]
-        return start(phase, group, send, recv, moves, (NF - 1, back[NF - 1]) if group == NEAR else None)
+    def over_columns(phase, group, send, recv):
+        moves = [
+            (k, COL_BACK[k], {"facet": other, "col": col_peers[k]}) for k in range(4 * group, 4 * group + 4)
+        ]
+        return start(phase, group, send, recv, moves)
+
+    def to_subgrids(phase, group, send, recv):
+        moves = [
+            (k, FACET_CROSS_BACK[k], {"facet": facet_peers[k]})
+            for k in range(8 * group, 8 * group + 8)
+            if k < NF - 1
+        ]
+        own = (NF - 1, FACET_CROSS_BACK[NF - 1]) if group == NEAR else None
+        return start(phase, group, send, recv, moves, own)
 
     def to_facets(phase, group, send, recv):
         moves, own = [], None
@@ -253,7 +257,7 @@
         for i in range(NI):
             for d in range(2):
                 put_left(uu, span(SLAB * i, SLAB), 256 * d, image[d, :, LJ * i:LJ * (i + 1)])
-        zs[...] = dot(uu[...], bm[...])
+        zs[...] = dot3(uu[...], bm[...])
         re = jnp.zeros((SLAB, LJ), F32)
         im = jnp.zeros((SLAB, LJ), F32)
         for i in range(NI):
@@ -277,22 +281,22 @@
                 )
             launch(g)
 
-    def row_products(vt, group, recv, targets):
+    def row_operand(group, recv):
         x = jnp.concatenate(unpack(recv[4 * group:4 * group + 4].reshape(32, 128)), axis=0)
         y = pltpu.roll(x, 32, 1)
         y = jnp.where(part == 0, y, -y)
-        return dot(vt[group, targets, :], right(jnp.concatenate([x, y], axis=0)))
-
-    def rows_forward(vt, waits, recv, phase, send, into, cross=True):
+        return right(jnp.concatenate([x, y], axis=0))
+
+    def rows_forward(waits, recv, phase, send, into):
         waits[NEAR].wait_recv()
-        near = row_products(vt, NEAR, recv, ALL)
-        zs[:, 0:128] = near
+        zs[:, 0:128] = dot3(vt[NEAR], row_operand(NEAR, recv))
         waits[FAR].wait_recv()
+        operand = row_operand(FAR, recv)
         later = []
         for g in range(2):
-            out = zs[span(256 * g, 256), 0:128] + row_products(vt, FAR, recv, span(256 * g, 256))
+            out = zs[span(256 * g, 256), 0:128] + dot3(vt[FAR, span(256 * g, 256), :], operand)
             send[8 * g:8 * g + 8] = jnp.where(low, out[0:128], out[128:256]).reshape(8, SLAB, 128)
-            later.append(to_subgrids(phase, g, send, into, cross))
+            later.append(to_subgrids(phase, g, send, into))
         return later
 
     loads[3].wait()
@@ -321,7 +325,7 @@
                 vc, vs = turns(rlane * (rows[facet_peers[a]] + 512 * (2 * p16 + h)), 16, vscale)
                 r0 = 256 * (a // 8) + 128 * h + SLAB * (a % 8)
                 put_left(vt.at[g], span(r0, SLAB), 0, jnp.where(low, vc, vs))
-    wait2 = rows_forward(vt, wait1, recv1, 1, send2, recv2)
+    wait2 = rows_forward(wait1, recv1, 1, send2, recv2)
 
     for d in range(0, M, SLAB):
         wc, ws = turns((d + iota((SLAB, G), 0)) * iota((SLAB, G), 1), 8, 1.0 / 16)
@@ -375,7 +379,7 @@
         put_right(rt.at[h], 0, span(256, 256), ri)
         put_right(rt.at[h], 128, span(0, 256), -ri)
         put_right(rt.at[h], 128, span(256, 256), rr)
-        zs[span(256 * h, 256), :] = dot(pk[span(256 * h, 256), :], rt[h])
+        zs[span(256 * h, 256), :] = dot3(pk[span(256 * h, 256), :], rt[h])
     wait3 = []
     for g in range(2):
         for h in range(2):
@@ -388,7 +392,7 @@
                 ws = tf[1, 8 * g + k:8 * g + k + 1, :]
                 put_left(uu, dst, 0, wc * zr - ws * zi)
                 put_left(uu, dst, 256, wc * zi + ws * zr)
-        out = dot(uu[span(256 * g, 256), :], wt[...])
+        out = dot3(uu[span(256 * g, 256), :], wt[...])
         send3[8 * g:8 * g + 8] = jnp.where(low, out[0:128], out[128:256]).reshape(8, SLAB, 128)
         wait3.append(to_facets(2, g, send3, recv3))
 
@@ -417,9 +421,9 @@
         put_right(half, 128 + r1, span(256, 256), bc)
 
     wait3[NEAR].wait_recv()
-    zs[:, 0:128] = dot(vb[NEAR], right(recv3[8:16].reshape(128, 128)))
+    zs[:, 0:128] = dot3(vb[NEAR], right(recv3[8:16].reshape(128, 128)))
     wait3[FAR].wait_recv()
-    out = zs[:, 0:128] + dot(vb[FAR], right(recv3[0:8].reshape(128, 128)))
+    out = zs[:, 0:128] + dot3(vb[FAR], right(recv3[0:8].reshape(128, 128)))
     dd = jnp.where(low, out[0:128], out[128:256])
     ee = jnp.where(low, out[256:384], out[384:512])
     dd = dd + pltpu.roll(dd, 64, 1)
@@ -450,7 +454,7 @@
             ws = at[1, i:i + 1, span(128 * g, 128)]
             put_left(ud, span(SLAB * i, SLAB), 0, sre * wc - sim * ws)
             put_left(ud, span(SLAB * i, SLAB), 128, sim * wc + sre * ws)
-        return dot(ud[...], bt[g])
+        return dot3(ud[...], bt[g])
 
     wait4[NEAR].wait_recv()
     near = columns_back(NEAR)
@@ -473,7 +477,7 @@
 
     wait5 = []
     columns_forward(new, send5, lambda g: wait5.append(over_columns(4, g, send5, recv5)))
-    wait6 = rows_forward(vt, wait5, recv5, 5, send6, recv6)
+    wait6 = rows_forward(wait5, recv5, 5, send6, recv6)
     wait6[NEAR].wait_recv()
     for h, x in enumerate(model_half(NEAR, recv6[8:16], wz, tf, pt, zs, tt)):
         gs[span(256 * h, 256), :] = x
@@ -491,7 +495,7 @@
     large = pltpu.VMEM((NF, SLAB, 128), F32)
 
     def left(rows, columns, *lead):
-        return pltpu.VMEM((*lead, rows, 3 * columns), BF16)
+        return pltpu.VMEM((*lead, rows, 2 * columns), BF16)
 
     def right_of(rows, columns, *lead):
         return pltpu.VMEM((*lead, 3 * rows, columns), BF16)

time: 41.8 us -> 41.5 us (level)
  no operation moved by 1% of the time
where the time goes in v4:
time: 41.5 us; the launch traced here: 41.4 us
  Pallas kernels  40.7 us (98%)
  between operations  0.64 us (2%)
    pallas_call x1, Pallas kernels, local(): pl.pallas_call(kernel, out_shape=(pltpu.VMEM((8, SLAB, 128), F32), pltpu....  39.2 us
    pallas_call x1, Pallas kernels, local(): pl.pallas_call(finish_kernel, out_shape=(jax.ShapeDtypeStruct((2, SLAB, F...  1.53 us

profile of v4, /device:TPU:1, one launch (start us, length us, event | category | flops | bytes accessed | tf_op | source)
XLA Modules:
  0.0 41.4 jit_solution(7945788044893029024)
XLA Ops:
  0.6 39.2 %imaging.1 = (f32[8,16,128]{2,1,0:T(8,128)S(1)}, f32[512,512]{1,0:T(8,128)S(1)}, bf16[256,512]{1,0:T(8,128)(2,1)S(1)}, f32[2,16,256]{2,1,0:T(8,128)S(1)}, bf16[2...) custom-call(s32[2,16]{1,0:T(2,128)} %bitcast.1, s32[16]{0:T(128)} %rows_h.1, s32[8]{0:T(128)} %cols_h.1, ...), custom_call_target="tpu_custom_call" | custom-call | tf_op jit(solution)/shard_map/imaging/pallas_call | solution.py:508
  39.9 1.5 %finish.1 = (f32[2,16,8192]{2,1,0:T(8,128)}, f32[2,256,256]{2,1,0:T(8,128)}) custom-call(f32[8,16,128]{2,1,0:T(8,128)S(1)} %get-tuple-element.8.parts, f32[512,512]{1,0:T(8,128)S(1)} %get-tuple-element.9.gs, bf16[256,512]{1,0:T(8,128)(2,1)S(1)} %get-tuple-element.10.wz, f32[2,16,256]{2,1,0:T(8,128)S(1)} %get-tuple-element.11.tf, ...), custom_call_target="tpu_custom_call" | custom-call | tf_op jit(solution)/shard_map/finish/pallas_call | solution.py:549

commit v5 on v4

--- a/solution.py
+++ b/solution.py
@@ -167,7 +167,7 @@
     loads = [
         pltpu.make_async_copy(src, dst, isem.at[n])
         for n, (src, dst) in enumerate(
-            ((cols_h, cols), (offs_h, offs), (rows_h, rows), (sky_h, sky), (obs_h, obs), (wts_h, wts))
+            ((sky_h, sky), (cols_h, cols), (offs_h, offs), (rows_h, rows), (obs_h, obs), (wts_h, wts))
         )
     ]
     for cp in loads:
@@ -233,7 +233,7 @@
 
     l256 = iota((1, LJ), 1)
     cv = 8 * (l256 & 31)
-    loads[0].wait()
+    loads[1].wait()
     for b in range(NC):
         cv = cv + jnp.where((l256 >> 5) == b, cols[col_peers[b]], 0)
     steps = iota((SLAB, LJ), 0)
@@ -246,17 +246,14 @@
         put_right(bm, SLAB * k, span(256, 256), -bs)
         put_right(bm, 256 + SLAB * k, span(0, 256), bs)
         put_right(bm, 256 + SLAB * k, span(256, 256), bc)
-    loads[1].wait()
+    loads[2].wait()
     s_me = offs[0, other]
     t_me = offs[1, f]
     ac, as_ = turns((t_me * FN + LJ * iota((NI, LJ), 0)) * cv, 16, 1.0 / math.sqrt(FN))
     at[0] = ac
     at[1] = as_
 
-    def columns_forward(image, send, launch):
-        for i in range(NI):
-            for d in range(2):
-                put_left(uu, span(SLAB * i, SLAB), 256 * d, image[d, :, LJ * i:LJ * (i + 1)])
+    def columns_forward(send, launch):
         zs[...] = dot3(uu[...], bm[...])
         re = jnp.zeros((SLAB, LJ), F32)
         im = jnp.zeros((SLAB, LJ), F32)
@@ -299,7 +296,7 @@
             later.append(to_subgrids(phase, g, send, into))
         return later
 
-    loads[3].wait()
+    loads[0].wait()
     wait1 = []
 
     def launch1(g):
@@ -307,9 +304,12 @@
             pl.semaphore_wait(barrier, NF - 1 + NC - 1)
         wait1.append(over_columns(0, g, send1, recv1))
 
-    columns_forward(sky, send1, launch1)
-
-    loads[2].wait()
+    for i in range(NI):
+        for d in range(2):
+            put_left(uu, span(SLAB * i, SLAB), 256 * d, sky[d, :, LJ * i:LJ * (i + 1)])
+    columns_forward(send1, launch1)
+
+    loads[3].wait()
 
     p16 = iota((SLAB, 128), 0)
     l128 = iota((SLAB, 128), 1)
@@ -396,19 +396,20 @@
         send3[8 * g:8 * g + 8] = jnp.where(low, out[0:128], out[128:256]).reshape(8, SLAB, 128)
         wait3.append(to_facets(2, g, send3, recv3))
 
-    r0 = iota((FROWS, 128), 0)
-    slab = jnp.zeros((FROWS, 128), jnp.int32)
-    for k in range(NC):
-        slab = jnp.where(((r0 >> 3) & 7) == k, col_peers[k], slab)
-    rcol = s_me * FN + SLAB * slab + 8 * (r0 >> 6) + (r0 & 7)
-    for g in range(2):
-        fl = 1024 * (lane & 15)
-        for k in range(8):
-            fl = fl + jnp.where((lane >> 4) == k, rows[facet_peers[8 * g + k]], 0)
-        for h in range(2):
-            vc, vs = turns(rcol * (fl + 512 * h), 16, vscale)
-            put_left(vb.at[g], span(128 * h, 128), 0, vc)
-            put_left(vb.at[g], span(256 + 128 * h, 128), 0, vs)
+    r0 = iota((64, 128), 0)
+    for t in range(2):
+        slab = jnp.zeros((64, 128), jnp.int32)
+        for k in range(4):
+            slab = jnp.where(((r0 >> 3) & 3) == k, col_peers[4 * t + k], slab)
+        rcol = s_me * FN + SLAB * slab + 8 * (r0 >> 5) + (r0 & 7)
+        for g in range(2):
+            fl = 1024 * (lane & 15)
+            for k in range(8):
+                fl = fl + jnp.where((lane >> 4) == k, rows[facet_peers[8 * g + k]], 0)
+            for h in range(2):
+                vc, vs = turns(rcol * (fl + 512 * h), 16, vscale)
+                put_left(vb.at[g], span(256 * t + 64 * h, 64), 0, vc)
+                put_left(vb.at[g], span(256 * t + 128 + 64 * h, 64), 0, vs)
     j256 = iota((M, LJ), 1)
     q32 = iota((M, LJ), 0)
     for b in range(NC):
@@ -423,15 +424,18 @@
     wait3[NEAR].wait_recv()
     zs[:, 0:128] = dot3(vb[NEAR], right(recv3[8:16].reshape(128, 128)))
     wait3[FAR].wait_recv()
-    out = zs[:, 0:128] + dot3(vb[FAR], right(recv3[0:8].reshape(128, 128)))
-    dd = jnp.where(low, out[0:128], out[128:256])
-    ee = jnp.where(low, out[256:384], out[384:512])
-    dd = dd + pltpu.roll(dd, 64, 1)
-    ee = ee + pltpu.roll(ee, 64, 1)
-    ee = pltpu.roll(ee, 32, 1)
-    dd = dd + jnp.where(part == 0, -ee, ee)
-    send4[...] = jnp.where(low, dd[0:64], dd[64:128]).reshape(NC, 8, 128)
-    wait4 = [over_columns(3, g, send4, recv4) for g in range(2)]
+    operand = right(recv3[0:8].reshape(128, 128))
+    wait4 = []
+    for t in range(2):
+        out = zs[span(256 * t, 256), 0:128] + dot3(vb[FAR, span(256 * t, 256), :], operand)
+        dd = jnp.where(low, out[0:64], out[64:128])
+        ee = jnp.where(low, out[128:192], out[192:256])
+        dd = dd + pltpu.roll(dd, 64, 1)
+        ee = ee + pltpu.roll(ee, 64, 1)
+        ee = pltpu.roll(ee, 32, 1)
+        dd = dd + jnp.where(part == 0, -ee, ee)
+        send4[4 * t:4 * t + 4] = jnp.where(low, dd[0:32], dd[32:64]).reshape(4, 8, 128)
+        wait4.append(over_columns(3, t, send4, recv4))
 
     def columns_back(g):
         x4 = jnp.concatenate(unpack(recv4[4 * g:4 * g + 4].reshape(32, 128)), axis=0)
@@ -472,11 +476,12 @@
         ui = new[1, :, LJ * i:LJ * (i + 1)] + zs[rs, 256:512]
         mag = jnp.sqrt(ur * ur + ui * ui)
         ratio = jnp.maximum(mag - SHRINK, 0.0) / jnp.maximum(mag, SHRINK)
-        new[0, :, LJ * i:LJ * (i + 1)] = ur * ratio
-        new[1, :, LJ * i:LJ * (i + 1)] = ui * ratio
+        for d, x in enumerate((ur * ratio, ui * ratio)):
+            new[d, :, LJ * i:LJ * (i + 1)] = x
+            put_left(uu, rs, 256 * d, x)
 
     wait5 = []
-    columns_forward(new, send5, lambda g: wait5.append(over_columns(4, g, send5, recv5)))
+    columns_forward(send5, lambda g: wait5.append(over_columns(4, g, send5, recv5)))
     wait6 = rows_forward(wait5, recv5, 5, send6, recv6)
     wait6[NEAR].wait_recv()
     for h, x in enumerate(model_half(NEAR, recv6[8:16], wz, tf, pt, zs, tt)):

time: 41.5 us -> 41.5 us (level)
  no operation moved by 1% of the time
where the time goes in v5:
time: 41.5 us; the launch traced here: 41.4 us
  Pallas kernels  40.8 us (98%)
  between operations  0.64 us (2%)
    pallas_call x1, Pallas kernels, local(): pl.pallas_call(kernel, out_shape=(pltpu.VMEM((8, SLAB, 128), F32), pltpu....  39.2 us
    pallas_call x1, Pallas kernels, local(): pl.pallas_call(finish_kernel, out_shape=(jax.ShapeDtypeStruct((2, SLAB, F...  1.53 us

profile of v5, /device:TPU:1, one launch (start us, length us, event | category | flops | bytes accessed | tf_op | source)
XLA Modules:
  0.0 41.4 jit_solution(2267289299906390229)
XLA Ops:
  0.6 39.2 %imaging.1 = (f32[8,16,128]{2,1,0:T(8,128)S(1)}, f32[512,512]{1,0:T(8,128)S(1)}, bf16[256,512]{1,0:T(8,128)(2,1)S(1)}, f32[2,16,256]{2,1,0:T(8,128)S(1)}, bf16[2...) custom-call(s32[2,16]{1,0:T(2,128)} %bitcast.1, s32[16]{0:T(128)} %rows_h.1, s32[8]{0:T(128)} %cols_h.1, ...), custom_call_target="tpu_custom_call" | custom-call | tf_op jit(solution)/shard_map/imaging/pallas_call | solution.py:513
  39.9 1.5 %finish.1 = (f32[2,16,8192]{2,1,0:T(8,128)}, f32[2,256,256]{2,1,0:T(8,128)}) custom-call(f32[8,16,128]{2,1,0:T(8,128)S(1)} %get-tuple-element.8.parts, f32[512,512]{1,0:T(8,128)S(1)} %get-tuple-element.9.gs, bf16[256,512]{1,0:T(8,128)(2,1)S(1)} %get-tuple-element.10.wz, f32[2,16,256]{2,1,0:T(8,128)S(1)} %get-tuple-element.11.tf, ...), custom_call_target="tpu_custom_call" | custom-call | tf_op jit(solution)/shard_map/finish/pallas_call | solution.py:554
